TPU v7x, 16 devices: a 4x2x1 block of a 4x4x8 slice. The times are simulated.
16 devices in a mesh: rep: 4 (over y, z, core), dp: 4 (over x).
Axes of the slice: x: 4, y: 2, z: 1, core: 2. Of those that a mesh axis runs over, the one named last changes fastest.
The devices are a block of a 4x4x8 slice.
Arguments:
- x: bfloat16 [16, 4096, 512], P(('rep', 'dp')), parts along dimension 0
- dy: bfloat16 [16, 4096, 512], P(('rep', 'dp')), parts along dimension 0
- w_gate: bfloat16 [2, 512, 1664], replicated
- w_up: bfloat16 [2, 512, 1664], replicated
- w_down: bfloat16 [2, 1664, 512], replicated
- m_w_gate: float32 [2, 512, 1664], replicated
- m_w_up: float32 [2, 512, 1664], replicated
- m_w_down: float32 [2, 1664, 512], replicated
- v_w_gate: float32 [2, 512, 1664], replicated
- v_w_up: float32 [2, 512, 1664], replicated
- v_w_down: float32 [2, 1664, 512], replicated
Outputs:
- output 1: bfloat16 [8, 512, 1664], P('rep'), parts along dimension 0
- output 2: bfloat16 [8, 512, 1664], P('rep'), parts along dimension 0
- output 3: bfloat16 [8, 1664, 512], P('rep'), parts along dimension 0
- output 4: float32 [8, 512, 1664], P('rep'), parts along dimension 0
- output 5: float32 [8, 512, 1664], P('rep'), parts along dimension 0
- output 6: float32 [8, 1664, 512], P('rep'), parts along dimension 0
- output 7: float32 [8, 512, 1664], P('rep'), parts along dimension 0
- output 8: float32 [8, 512, 1664], P('rep'), parts along dimension 0
- output 9: float32 [8, 1664, 512], P('rep'), parts along dimension 0
There are 4 independent parts. A program takes and returns all parts, laid end to end along the dimension named above; an argument that names none is the same for every part.
All inputs are finite; a program needn't handle non-finite values.
Results may differ from a plain program's by a relative error of at most 0.022.
Values are sent between devices in bfloat16 or wider.
A program may use at most 768 MiB of HBM per device.

v0:
```python
import jax
import jax.numpy as jnp
from jax import lax
from jax.sharding import PartitionSpec as P

NAMES = ("w_gate", "w_up", "w_down")


def matmul(a, w):
    return jnp.dot(a, w, preferred_element_type=jnp.float32).astype(jnp.bfloat16)


def normed(h):
    wide = h.astype(jnp.float32)
    scale = lax.rsqrt(jnp.mean(wide**2, -1, keepdims=True) + 1e-6)
    return (wide * scale).astype(jnp.bfloat16)


def layer(h, w):
    a = normed(h)
    gate = jnp.dot(a, w["w_gate"], preferred_element_type=jnp.float32)
    up = jnp.dot(a, w["w_up"], preferred_element_type=jnp.float32)
    return h + matmul((jax.nn.silu(gate) * up).astype(jnp.bfloat16), w["w_down"])


def adamw(w, m, v, g):
    m = 0.9 * m + 0.1 * g
    v = 0.95 * v + 0.05 * g * g
    step = m * lax.rsqrt(v + 1e-8) + 0.1 * w
    return (w - 0.02 * step).astype(jnp.bfloat16), m, v


def clipped(gradients, sum_of_squares, count):
    factor = jnp.minimum(1.0, 0.5 * lax.rsqrt(sum_of_squares / count + 1e-30))
    return [g * factor for g in gradients]


def solution(mesh):
    def step(x, dy, *arrays):
        weights, m, v = (arrays[i : i + 3] for i in (0, 3, 6))
        layers = weights[0].shape[0]
        h, kept = x[0], []
        for number in range(layers):
            kept.append(h)
            h = layer(h, {name: w[number] for name, w in zip(NAMES, weights, strict=True)})
        by_h, summed = dy[0], [None] * layers
        for number in reversed(range(layers)):
            _, back = jax.vjp(lambda w, h: layer(h, w), {name: w[number] for name, w in zip(NAMES, weights, strict=True)}, kept[number])
            by_w, by_h = back(by_h)
            summed[number] = [lax.psum(by_w[name], "dp") for name in NAMES]
        gradients = [jnp.stack([summed[number][i] for number in range(layers)]).astype(jnp.float32) for i in range(3)]
        gradients = clipped(gradients, sum(jnp.sum(g * g) for g in gradients), sum(g.size for g in gradients))
        new = [adamw(w.astype(jnp.float32), m, v, g) for w, m, v, g in zip(weights, m, v, gradients, strict=True)]
        return tuple(one[which] for which in range(3) for one in new)

    return jax.shard_map(
        step,
        mesh=mesh,
        in_specs=(P(("rep", "dp"), None, None),) * 2 + (P(None, None, None),) * 9,
        out_specs=(P("rep", None, None),) * 9,
        check_vma=False,
    )
```

profile of v0, /device:TPU:112, one launch (start us, length us, event | category | flops | bytes accessed | tf_op | source)
XLA Modules:
  0.0 539.4 jit_solution(3287508339615919864)
XLA Ops:
  7.3 6.3 %copy.20 = bf16[1,4096,512]{1,2,0:T(8,128)(2,1)} copy(bf16[1,4096,512]{2,1,0:T(8,128)(2,1)} %param.11) | data formatting | bytes 8388608 | tf_op args[0]
  13.6 3.2 fusion.15
  16.8 6.3 %copy.21 = bf16[1,4096,512]{1,2,0:T(8,128)(2,1)} copy(bf16[1,4096,512]{2,1,0:T(8,128)(2,1)} %param.12) | data formatting | bytes 8388608 | tf_op args[1]
  23.2 12.5 %convolution_convert_fusion.1 = bf16[4096,1664]{1,0:T(8,128)(2,1)} fusion(bf16[1,4096,512]{2,1,0:T(8,128)(2,1)} %param.12, bf16[2,1664,512]{2,1,0:T(8,128)(2,1)S(1)} %copy-done.9), kind=kOutput, calls=%fused_computation.23 | convolution fusion | flops 6986137600 | bytes 19529728 | tf_op jit(solution)/shard_map/transpose(jvp())/dot_general | solution.py:10
  35.7 13.0 %fusion.94 = f32[4096,1664]{1,0:T(8,128)} fusion(bf16[2,512,1664]{2,1,0:T(8,128)(2,1)S(1)} %copy-done.11, bf16[1,4096,512]{2,1,0:T(8,128)(2,1)S(1)} %copy-done.5, f32[4096]{0:T(1024)S(1)} %add_rsqrt_fusion), kind=kOutput, calls=%fused_computation.112 | convolution fusion | flops 6985613312 | bytes 33177600 | tf_op jit(solution)/shard_map/dot_general | solution.py:21
  48.7 27.4 %multiply_convert_fusion.1 = (bf16[4096,1664]{1,0:T(8,128)(2,1)}, f32[4096,1664]{1,0:T(8,128)}) fusion(f32[4096,1664]{1,0:T(8,128)} %fusion.94, bf16[2,512,1664]{2,1,0:T(8,128)(2,1)} %param.14, bf16[1,4096,512]{2,1,0:T(8,128)(2,1)} %param.11, f32[4096]{0:T(1024)S(1)} %add_rsqrt_fusion), kind=kOutput, calls=%fused_computation.17 | convolution fusion | flops 7026507776 | bytes 74072064 | tf_op jit(solution)/shard_map/dot_general | solution.py:22
  76.2 12.5 %fusion.19 = (f32[4096]{0:T(1024)S(1)}, bf16[4096,512]{0,1:T(8,128)(2,1)S(1)}) fusion(bf16[4096,1664]{1,0:T(8,128)(2,1)} %get-tuple-element.24, bf16[2,1664,512]{2,1,0:T(8,128)(2,1)S(1)} %copy-done.9, bf16[1,4096,512]{1,2,0:T(8,128)(2,1)} %copy.20), kind=kOutput, calls=%fused_computation.52 | convolution fusion | flops 6989803520 | bytes 23740416 | tf_op jit(solution)/shard_map/dot_general | solution.py:10
  90.7 13.0 %fusion.81 = f32[4096,1664]{1,0:T(8,128)} fusion(bf16[4096,512]{0,1:T(8,128)(2,1)S(1)} %get-tuple-element.27, f32[4096]{0:T(1024)S(1)} %fusion.107, bf16[2,512,1664]{2,1,0:T(8,128)(2,1)S(1)} %copy-done.14), kind=kOutput, calls=%fused_computation.101 | convolution fusion | flops 6985613312 | bytes 33177600 | tf_op jit(solution)/shard_map/jvp()/dot_general | solution.py:22
  103.7 34.2 %fusion.2 = (bf16[4096,1664]{1,0:T(8,128)(2,1)}, f32[4096,1664]{1,0:T(8,128)}) fusion(f32[4096,1664]{1,0:T(8,128)} %fusion.81, bf16[4096,1664]{1,0:T(8,128)(2,1)} %convolution_convert_fusion.1, bf16[2,512,1664]{2,1,0:T(8,128)(2,1)} %param.13, bf16[4096,512]{0,1:T(8,128)(2,1)} %copy-done.7, f32[4096]{0:T(1024)S(1)} %fusion.107), kind=kOutput, calls=%fused_computation.8 | convolution fusion | flops 7067402240 | bytes 87703552 | tf_op jit(solution)/shard_map/jvp()/dot_general | solution.py:21
  137.9 20.5 %fusion.65 = bf16[1,1664,512]{2,1,0:T(8,128)(2,1)} fusion(bf16[1,4096,512]{2,1,0:T(8,128)(2,1)S(1)} %copy-done.6, f32[4096,1664]{1,0:T(8,128)} %fusion.81, f32[4096,1664]{1,0:T(8,128)} %get-tuple-element.29), kind=kOutput, calls=%fused_computation.95 | convolution fusion | flops 7021068288 | bytes 60424192 | tf_op jit(solution)/shard_map/transpose(jvp())/dot_general | solution.py:10
  158.4 19.9 %fusion.69 = bf16[1,512,1664]{2,1,0:T(8,128)(2,1)} fusion(bf16[4096,1664]{1,0:T(8,128)(2,1)} %convolution_convert_fusion.1, bf16[4096,512]{0,1:T(8,128)(2,1)} %copy-done.7, f32[4096]{0:T(1024)S(1)} %fusion.107, f32[4096,1664]{1,0:T(8,128)} %get-tuple-element.29), kind=kOutput, calls=%fused_computation.97 | convolution fusion | flops 7027359744 | bytes 46809088 | tf_op jit(solution)/shard_map/transpose(jvp())/dot_general | solution.py:22
  178.3 19.3 %fusion.43 = bf16[4096,512]{0,1:T(8,128)(2,1)} fusion(bf16[4096,1664]{1,0:T(8,128)(2,1)} %convolution_convert_fusion.1, bf16[2,512,1664]{2,1,0:T(8,128)(2,1)S(1)} %copy-done.15, f32[4096,1664]{1,0:T(8,128)} %get-tuple-element.29), kind=kOutput, calls=%fused_computation.77 | convolution fusion | flops 7022313472 | bytes 46792704 | tf_op jit(solution)/shard_map/transpose(jvp())/dot_general | solution.py:22
  197.6 14.5 %fusion.75 = bf16[1,512,1664]{2,1,0:T(8,128)(2,1)} fusion(bf16[4096,1664]{1,0:T(8,128)(2,1)} %get-tuple-element.28, bf16[4096,512]{0,1:T(8,128)(2,1)} %copy-done.7, f32[4096]{0:T(1024)S(1)} %fusion.107), kind=kOutput, calls=%fused_computation.99 | convolution fusion | flops 6985613312 | bytes 19546112 | tf_op jit(solution)/shard_map/transpose(jvp())/dot_general | solution.py:21
  212.1 12.1 %fusion.21 = (f32[4096]{0:T(1024)S(1)}, bf16[4096,512]{0,1:T(8,128)(2,1)S(1)}) fusion(bf16[4096,512]{0,1:T(8,128)(2,1)S(1)} %copy-done.8, bf16[4096,512]{0,1:T(8,128)(2,1)} %fusion.43, bf16[4096,1664]{1,0:T(8,128)(2,1)} %get-tuple-element.28, bf16[2,512,1664]{2,1,0:T(8,128)(2,1)S(1)} %copy-done.12), kind=kOutput, calls=%fused_computation.54 | convolution fusion | flops 6989803520 | bytes 27934720 | tf_op jit(solution)/shard_map/transpose(jvp())/dot_general | solution.py:21
  224.3 3.1 fusion.48
  227.5 12.3 %fusion.68 = bf16[1,1664,512]{2,1,0:T(8,128)(2,1)} fusion(bf16[4096,1664]{1,0:T(8,128)(2,1)} %get-tuple-element.24, bf16[4096,512]{0,1:T(8,128)(2,1)S(1)} %fusion.48), kind=kOutput, calls=%fused_computation.96 | convolution fusion | flops 6980173824 | bytes 19529728 | tf_op jit(solution)/shard_map/transpose(jvp())/dot_general | solution.py:10
  239.8 10.9 %convolution_convert_fusion = bf16[4096,1664]{1,0:T(8,128)(2,1)} fusion(bf16[4096,512]{0,1:T(8,128)(2,1)S(1)} %fusion.48, bf16[2,1664,512]{2,1,0:T(8,128)(2,1)S(1)} %copy-done.10), kind=kOutput, calls=%fused_computation.22 | convolution fusion | flops 6986137600 | bytes 19529728 | tf_op jit(solution)/shard_map/transpose(jvp())/dot_general | solution.py:10
  250.6 20.0 %fusion.76 = bf16[1,512,1664]{2,1,0:T(8,128)(2,1)} fusion(bf16[4096,1664]{1,0:T(8,128)(2,1)} %convolution_convert_fusion, f32[4096,1664]{1,0:T(8,128)} %fusion.94, bf16[1,4096,512]{1,2,0:T(8,128)(2,1)} %copy.20, f32[4096]{0:T(1024)S(1)} %copy-done.20), kind=kOutput, calls=%fused_computation.100 | convolution fusion | flops 7027359744 | bytes 46809088 | tf_op jit(solution)/shard_map/transpose(jvp())/dot_general | solution.py:22
  270.6 27.0 %fusion.70 = bf16[1,512,1664]{2,1,0:T(8,128)(2,1)} fusion(f32[4096,1664]{1,0:T(8,128)} %fusion.94, f32[4096,1664]{1,0:T(8,128)} %get-tuple-element.25, bf16[4096,1664]{1,0:T(8,128)(2,1)} %convolution_convert_fusion, bf16[1,4096,512]{1,2,0:T(8,128)(2,1)} %copy.20, f32[4096]{0:T(1024)S(1)} %copy-done.20), kind=kOutput, calls=%fused_computation.98 | convolution fusion | flops 7061438464 | bytes 74072064 | tf_op jit(solution)/shard_map/transpose(jvp())/dot_general | solution.py:21
  297.7 184.5 %all-reduce.3.cloned.1.call-done = (bf16[1,512,1664]{2,1,0:T(8,128)(2,1)}, bf16[1,512,1664]{2,1,0:T(8,128)(2,1)}, bf16[1,512,1664]{2,1,0:T(8,128)(2,1)}, bf16[1,...) async-done(((bf16[1,512,1664]{2,1,0:T(8,128)(2,1)}, bf16[1,512,1664]{2,1,0:T(8,128)(2,1)}, bf16[1,512,1664]{2,1,0:T(8,128)(2,1)}, ...) | async-done | bytes 10223632 | tf_op jit(solution)/shard_map/psum | solution.py:50
  482.2 4.5 fusion.33
  486.7 4.3 fusion.32
  495.4 14.4 %fusion.39 = (bf16[2,1664,512]{2,1,0:T(8,128)(2,1)}, f32[2,1664,512]{2,1,0:T(8,128)}, f32[2,1664,512]{2,1,0:T(8,128)}) fusion(bf16[2,1664,512]{2,1,0:T(8,128)(2,1)} %param.15, f32[]{:T(128)S(6)} %min_shard_map.3, bf16[1,1664,512]{2,1,0:T(8,128)(2,1)} %get-tuple-element.13, bf16[1,1664,512]{2,1,0:T(8,128)(2,1)} %get-tuple-element.14, ...), kind=kLoop, calls=%fused_computation.73 | loop fusion | flops 34078720 | bytes 37486596 | tf_op jit(solution)/shard_map/convert_element_type | solution.py:30
  511.1 21.1 %fusion.30 = (bf16[2,512,1664]{2,1,0:T(8,128)(2,1)}, f32[2,512,1664]{2,1,0:T(8,128)}, f32[2,512,1664]{2,1,0:T(8,128)}, bf16[2,512,1664]{2,1,0:T(8,128)(2,1)}, f3...) fusion(bf16[2,512,1664]{2,1,0:T(8,128)(2,1)S(1)} %copy-done.13, f32[]{:T(128)S(6)} %min_shard_map.3, ...), kind=kLoop, calls=%fused_computation.64 | loop fusion | flops 68157440 | bytes 74973184 | tf_op jit(solution)/shard_map/convert_element_type | solution.py:30
  (48 shorter events, 5.8 us)
Async XLA Ops:
  7.2 475.0 %all-reduce.3.cloned.1.call-start = ((), (), s32[]{:S(2)}) async-start(), calls=%async_computation | async-start | bytes 20447232 | tf_op jit(solution)/shard_map/psum | solution.py:50
  13.6 9.6 %copy-start.9 = (bf16[2,1664,512]{2,1,0:T(8,128)(2,1)S(1)}, bf16[2,1664,512]{2,1,0:T(8,128)(2,1)}, u32[]{:S(2)}) copy-start(bf16[2,1664,512]{2,1,0:T(8,128)(2,1)} %param.15) | copy-start | bytes 10223620
  16.8 31.9 %copy-start.19 = (f32[4096]{0:T(1024)}, f32[4096]{0:T(1024)S(1)}, u32[]{:S(2)}) copy-start(f32[4096]{0:T(1024)S(1)} %add_rsqrt_fusion) | copy-start | bytes 49156
  23.2 12.6 %copy-start.5 = (bf16[1,4096,512]{2,1,0:T(8,128)(2,1)S(1)}, bf16[1,4096,512]{2,1,0:T(8,128)(2,1)}, u32[]{:S(2)}) copy-start(bf16[1,4096,512]{2,1,0:T(8,128)(2,1)} %param.11) | copy-start | bytes 12582916
  23.2 12.6 %copy-start.11 = (bf16[2,512,1664]{2,1,0:T(8,128)(2,1)S(1)}, bf16[2,512,1664]{2,1,0:T(8,128)(2,1)}, u32[]{:S(2)}) copy-start(bf16[2,512,1664]{2,1,0:T(8,128)(2,1)} %param.13) | copy-start | bytes 10223620
  76.2 14.5 %copy-start.14 = (bf16[2,512,1664]{2,1,0:T(8,128)(2,1)S(1)}, bf16[2,512,1664]{2,1,0:T(8,128)(2,1)}, u32[]{:S(2)}) copy-start(bf16[2,512,1664]{2,1,0:T(8,128)(2,1)} %param.14) | copy-start | bytes 10223620
  88.7 2.0 copy-start.7
  88.7 2.0 copy-start.17
  103.7 34.2 %copy-start.6 = (bf16[1,4096,512]{2,1,0:T(8,128)(2,1)S(1)}, bf16[1,4096,512]{2,1,0:T(8,128)(2,1)}, u32[]{:S(2)}) copy-start(bf16[1,4096,512]{2,1,0:T(8,128)(2,1)} %param.12) | copy-start | bytes 12582916
  158.4 19.9 %copy-start.15 = (bf16[2,512,1664]{2,1,0:T(8,128)(2,1)S(1)}, bf16[2,512,1664]{2,1,0:T(8,128)(2,1)}, u32[]{:S(2)}) copy-start(bf16[2,512,1664]{2,1,0:T(8,128)(2,1)} %param.14) | copy-start | bytes 10223620
  197.6 14.5 %copy-start.8 = (bf16[4096,512]{0,1:T(8,128)(2,1)S(1)}, bf16[4096,512]{0,1:T(8,128)(2,1)}, u32[]{:S(2)}) copy-start(bf16[4096,512]{0,1:T(8,128)(2,1)} %copy-done.7) | copy-start | bytes 12582916
  197.6 14.5 %copy-start.12 = (bf16[2,512,1664]{2,1,0:T(8,128)(2,1)S(1)}, bf16[2,512,1664]{2,1,0:T(8,128)(2,1)}, u32[]{:S(2)}) copy-start(bf16[2,512,1664]{2,1,0:T(8,128)(2,1)} %param.13) | copy-start | bytes 10223620
  212.1 12.2 %copy-start.18 = (f32[4096]{0:T(1024)S(1)}, f32[4096]{0:T(1024)}, u32[]{:S(2)}) copy-start(f32[4096]{0:T(1024)} %copy-done.17) | copy-start | bytes 49156
  212.1 12.2 %copy-start = (bf16[1,4096,512]{1,2,0:T(8,128)(2,1)S(1)}, bf16[1,4096,512]{1,2,0:T(8,128)(2,1)}, u32[]{:S(2)}) copy-start(bf16[1,4096,512]{1,2,0:T(8,128)(2,1)} %copy.21) | copy-start | bytes 12582916
  227.4 12.3 %copy-start.10 = (bf16[2,1664,512]{2,1,0:T(8,128)(2,1)S(1)}, bf16[2,1664,512]{2,1,0:T(8,128)(2,1)}, u32[]{:S(2)}) copy-start(bf16[2,1664,512]{2,1,0:T(8,128)(2,1)} %param.15) | copy-start | bytes 10223620
  239.8 10.9 %copy-start.20 = (f32[4096]{0:T(1024)S(1)}, f32[4096]{0:T(1024)}, u32[]{:S(2)}) copy-start(f32[4096]{0:T(1024)} %copy-done.19) | copy-start | bytes 49156
  482.2 8.8 %copy-start.1 = (bf16[1,512,1664]{2,1,0:T(8,128)(2,1)S(1)}, bf16[1,512,1664]{2,1,0:T(8,128)(2,1)}, u32[]{:S(2)}) copy-start(bf16[1,512,1664]{2,1,0:T(8,128)(2,1)} %get-tuple-element.9) | copy-start | bytes 5111812
  482.2 8.8 %copy-start.2 = (bf16[1,512,1664]{2,1,0:T(8,128)(2,1)S(1)}, bf16[1,512,1664]{2,1,0:T(8,128)(2,1)}, u32[]{:S(2)}) copy-start(bf16[1,512,1664]{2,1,0:T(8,128)(2,1)} %get-tuple-element.10) | copy-start | bytes 5111812
  495.4 14.5 %copy-start.3 = (bf16[1,512,1664]{2,1,0:T(8,128)(2,1)S(1)}, bf16[1,512,1664]{2,1,0:T(8,128)(2,1)}, u32[]{:S(2)}) copy-start(bf16[1,512,1664]{2,1,0:T(8,128)(2,1)} %get-tuple-element.11) | copy-start | bytes 5111812
  495.4 14.5 %copy-start.4 = (bf16[1,512,1664]{2,1,0:T(8,128)(2,1)S(1)}, bf16[1,512,1664]{2,1,0:T(8,128)(2,1)}, u32[]{:S(2)}) copy-start(bf16[1,512,1664]{2,1,0:T(8,128)(2,1)} %get-tuple-element.12) | copy-start | bytes 5111812
  495.4 14.5 %copy-start.13 = (bf16[2,512,1664]{2,1,0:T(8,128)(2,1)S(1)}, bf16[2,512,1664]{2,1,0:T(8,128)(2,1)}, u32[]{:S(2)}) copy-start(bf16[2,512,1664]{2,1,0:T(8,128)(2,1)} %param.13) | copy-start | bytes 10223620
  495.4 15.7 %copy-start.16 = (bf16[2,512,1664]{2,1,0:T(8,128)(2,1)S(1)}, bf16[2,512,1664]{2,1,0:T(8,128)(2,1)}, u32[]{:S(2)}) copy-start(bf16[2,512,1664]{2,1,0:T(8,128)(2,1)} %param.14) | copy-start | bytes 10223620
Sparse Core Ops, SparseCore 0:
  297.8 184.3 all-reduce.2
where the time goes:
time: 547 us; the launch traced here: 539 us
  matrix products  269 us (49%)
  waiting for transfers between devices  185 us (34%)
  other arithmetic  53 us (10%)
  between operations  16.7 us (3%)
  local copies, waits for them, and re-layouts  15.9 us (3%)
    psum x1, waiting for transfers between devices, step(): summed[number] = [lax.psum(by_w[name], 'dp') for name in NAMES]  185 us
    dot_general x5, matrix products, layer(): gate = jnp.dot(a, w['w_gate'], preferred_element_type=jnp.float32)  101 us
    dot_general x5, matrix products, layer(): up = jnp.dot(a, w['w_up'], preferred_element_type=jnp.float32)  99.6 us
    dot_general x5, matrix products, matmul(): jnp.dot(a, w, preferred_element_type=jnp.float32).astype(jnp.bfloat16)  68.7 us
    convert_element_type x2, other arithmetic, adamw(): return ((w - 0.02 * step).astype(jnp.bfloat16), m, v)  35.5 us
    unnamed x44, local copies, waits for them, and re-layouts  15.9 us
    reduce_sum x3, other arithmetic, step(): jnp.sum(g * g)  11.1 us
  transfers between devices with their start and end apart: 1, of which 1 were waited for; matrix products, arithmetic and copies ran while one was open for 0% of the time, Pallas kernels for 0%

commit v1 on v0

v1 whole, which is shorter than its diff:
```python
import functools

import jax
import jax.numpy as jnp
from jax import lax
from jax.experimental import pallas as pl
from jax.experimental.pallas import tpu as pltpu
from jax.sharding import PartitionSpec as P

F32, BF16 = jnp.float32, jnp.bfloat16
MESH = pl.DeviceIdType.MESH
LANES = 128
VMEM_LIMIT = 67043328
TILE = 512
CHUNK = 2 * LANES


def by_columns(a, b):
    return lax.dot_general(a, b, (((1,), (1,)), ((), ())), preferred_element_type=F32)


def tokens_kernel(x_ref, dy_ref, wg_ref, wu_ref, wd_ref, dyt_ref, a1t_ref, dht_ref, a0t_ref, hid1_ref, dgu1_ref, hid0_ref, dgu0_ref,
                  wgu, wd, keep, sems, *, many):
    layers, ff, _ = wd.shape
    blocks = ff // LANES

    @pl.when(pl.program_id(0) == 0)
    def _():
        copies = []
        for n in range(layers):
            for k in range(blocks):
                for which, ref in enumerate((wg_ref, wu_ref)):
                    at = 2 * k + which
                    copies.append(pltpu.make_async_copy(
                        ref.at[n, :, pl.ds(k * LANES, LANES)], wgu.at[n, :, pl.ds(at * LANES, LANES)], sems.at[n, at]))
            copies.append(pltpu.make_async_copy(wd_ref.at[n], wd.at[n], sems.at[n, 2 * blocks]))
        for copy in copies:
            copy.start()
        for copy in copies:
            copy.wait()

    def scaled(h):
        wide = h.astype(F32)
        scale = lax.rsqrt(jnp.mean(wide * wide, -1, keepdims=True) + 1e-6)
        return wide, scale, (wide * scale).astype(BF16)

    def lane(k):
        return pl.ds(k * LANES, LANES)

    groups = [(k, min(many, blocks - k)) for k in range(0, blocks, many)]
    h0 = x_ref[...]
    _, _, a0 = scaled(h0)
    a0t_ref[...] = a0.T
    for k, count in groups:
        gu = jnp.dot(a0, wgu[0, :, pl.ds(2 * k * LANES, 2 * count * LANES)], preferred_element_type=F32)
        for i in range(count):
            g, u = (gu[:, (2 * i + j) * LANES : (2 * i + j + 1) * LANES] for j in range(2))
            s = 0.5 * jnp.tanh(0.5 * g) + 0.5
            silu = g * s
            hid0_ref[:, lane(k + i)] = (silu * u).astype(BF16)
            keep[:, lane(2 * (k + i))] = (s + silu * (1.0 - s)) * u
            keep[:, lane(2 * (k + i) + 1)] = silu
    h1 = h0 + jnp.dot(hid0_ref[...], wd[0], preferred_element_type=F32).astype(BF16)
    wide, scale, a1 = scaled(h1)
    a1t_ref[...] = a1.T
    dy = dy_ref[...]
    dyt_ref[...] = dy.T
    for k, count in groups:
        gu = jnp.dot(a1, wgu[1, :, pl.ds(2 * k * LANES, 2 * count * LANES)], preferred_element_type=F32)
        dhid = by_columns(dy, wd[1, pl.ds(k * LANES, count * LANES), :]).astype(BF16).astype(F32)
        for i in range(count):
            g, u = (gu[:, (2 * i + j) * LANES : (2 * i + j + 1) * LANES] for j in range(2))
            dh = dhid[:, i * LANES : (i + 1) * LANES]
            s = 0.5 * jnp.tanh(0.5 * g) + 0.5
            silu = g * s
            hid1_ref[:, lane(k + i)] = (silu * u).astype(BF16)
            dgu1_ref[:, lane(2 * (k + i))] = (dh * u * (s + silu * (1.0 - s))).astype(BF16)
            dgu1_ref[:, lane(2 * (k + i) + 1)] = (dh * silu).astype(BF16)
    da = by_columns(dgu1_ref[...], wgu[1]).astype(BF16).astype(F32)
    along = jnp.mean(da * wide, -1, keepdims=True)
    dh1 = dy + (scale * (da - wide * (scale * scale) * along)).astype(BF16)
    dht_ref[...] = dh1.T
    for k, count in groups:
        dhid = by_columns(dh1, wd[0, pl.ds(k * LANES, count * LANES), :]).astype(BF16).astype(F32)
        for i in range(count):
            dh = dhid[:, i * LANES : (i + 1) * LANES]
            for j in range(2):
                at = lane(2 * (k + i) + j)
                dgu0_ref[:, at] = (dh * keep[:, at]).astype(BF16)


def tokens_pass(x, dy, wg, wu, wd):
    _, tokens, d = x.shape
    layers, ff, _ = wd.shape
    tile = min(TILE, tokens)
    lead = pl.BlockSpec((None, tile, d), lambda i: (0, i, 0))
    hbm = pl.BlockSpec(memory_space=pl.ANY)
    turned = pl.BlockSpec((d, tile), lambda i: (0, i))
    widths = (ff, 2 * ff, ff, 2 * ff)
    return pl.pallas_call(
        functools.partial(tokens_kernel, many=2),
        grid=(tokens // tile,),
        out_shape=[jax.ShapeDtypeStruct((d, tokens), BF16)] * 4 + [jax.ShapeDtypeStruct((tokens, n), BF16) for n in widths],
        in_specs=[lead, lead, hbm, hbm, hbm],
        out_specs=[turned] * 4 + [pl.BlockSpec((tile, n), lambda i: (i, 0)) for n in widths],
        scratch_shapes=[
            pltpu.VMEM((layers, d, 2 * ff), BF16),
            pltpu.VMEM((layers, ff, d), BF16),
            pltpu.VMEM((tile, 2 * ff), F32),
            pltpu.SemaphoreType.DMA((layers, 2 * ff // LANES + 1)),
        ],
        compiler_params=pltpu.CompilerParams(vmem_limit_bytes=VMEM_LIMIT, dimension_semantics=("arbitrary",)),
        cost_estimate=pl.CostEstimate(flops=2 * 9 * tokens * d * ff, bytes_accessed=16 * tokens * ff, transcendentals=2 * tokens * ff),
        name="tokens",
    )(x, dy, wg, wu, wd)


(VIA_LEFT, VIA_RIGHT, OWN_LEFT, OWN_RIGHT, SUM_LEFT, SUM_RIGHT, ALL_LEFT, ALL_RIGHT, FAR_LEFT, FAR_RIGHT) = range(10)


def units_of(layers, ff):
    cut = (ff // LANES // 2) * LANES
    return [(down, n, start, size) for n in reversed(range(layers)) for down in (True, False) for start, size in ((0, cut), (cut, ff - cut))]


def reduce_kernel(n, dyt_ref, a1t_ref, dht_ref, a0t_ref, hid1_ref, dgu1_ref, hid0_ref, dgu0_ref, gd_out, gg_out, gu_out, sq_out,
                  lefts, rights, own_d, own_gu, via_d, via_gu, in_d, in_gu, all_d, all_gu, squares,
                  left_sem, right_sem, send, recv, sq_send, sq_recv, out_sem):
    layers, ff, d = own_d.shape
    units = units_of(layers, ff)
    me = lax.axis_index("dp")
    right, left, far = lax.rem(me + 1, n), lax.rem(me + n - 1, n), lax.rem(me + n // 2, n)

    barrier = pltpu.get_barrier_semaphore()
    for step in range(1, n):
        pl.semaphore_signal(barrier, inc=1, device_id={"dp": lax.rem(me + step, n)}, device_id_type=MESH)

    def share(ref, unit, owner, half):
        down, layer, start, size = unit
        rows = (size if down else d) // n
        first = owner * rows
        if half is not None:
            rows = rows // 2
            first = first + half * rows
        if down:
            return ref[0].at[layer, pl.ds(pl.multiple_of(start + first, 16), rows), :]
        return ref[1].at[layer, :, pl.ds(pl.multiple_of(first, 16), rows), pl.ds(start, size)]

    def slot(ref, unit, k):
        down, layer, start, size = unit
        if down:
            return ref[0].at[k, layer, pl.ds(start // (2 * n), size // (2 * n)), :]
        return ref[1].at[k, layer, :, :, pl.ds(start, size)]

    own, via, arrived, whole = (own_d, own_gu), (via_d, via_gu), (in_d, in_gu), (all_d, all_gu)

    def remote(u, kind):
        unit = units[u]
        to = left if kind % 2 == 0 else right
        if kind in (VIA_LEFT, VIA_RIGHT):
            src, dst = share(own, unit, far, kind - VIA_LEFT), slot(via, unit, kind - VIA_LEFT)
        elif kind in (OWN_LEFT, OWN_RIGHT):
            src, dst = share(own, unit, to, 1 if kind == OWN_LEFT else 0), slot(arrived, unit, 1 if kind == OWN_LEFT else 0)
        elif kind in (SUM_LEFT, SUM_RIGHT):
            src, dst = share(own, unit, to, kind - SUM_LEFT), slot(arrived, unit, 2 + kind - SUM_LEFT)
        elif kind in (ALL_LEFT, ALL_RIGHT):
            src = dst = share(whole, unit, me, None)
        else:
            src = dst = share(whole, unit, right if kind == FAR_LEFT else left, 1 if kind == FAR_LEFT else 0)
        return pltpu.make_async_remote_copy(src_ref=src, dst_ref=dst, send_sem=send.at[u, kind], recv_sem=recv.at[u, kind],
                                            device_id={"dp": to}, device_id_type=MESH)

    def start(u, *kinds):
        for kind in kinds:
            remote(u, kind).start()

    def arrive(u, *kinds):
        for kind in kinds:
            remote(u, kind).wait_recv()

    def each(unit, body):
        down, _, _, size = unit
        blocks = (size if down else d) // (2 * n) // 16
        for which in range(1 if down else 2):
            def one(i, _, which=which):
                rows = pl.ds(pl.multiple_of(i * 16, 16), 16)
                body((rows, slice(None)) if down else (which, rows, slice(None)))
                return 0

            lax.fori_loop(0, blocks, one, 0)

    def forward_sums(u):
        unit = units[u]
        for k, kind, owner in ((0, SUM_LEFT, left), (1, SUM_RIGHT, right)):
            arrive(u, VIA_LEFT + k)
            mine, other = share(own, unit, owner, k), slot(via, unit, k)

            def add(at, mine=mine, other=other):
                mine[at] = (mine[at].astype(F32) + other[at].astype(F32)).astype(BF16)

            each(unit, add)
            start(u, kind)

    def finish(u):
        unit = units[u]
        arrive(u, OWN_LEFT, OWN_RIGHT, SUM_LEFT, SUM_RIGHT)
        for half in range(2):
            mine, out = share(own, unit, me, half), share(whole, unit, me, half)
            one, two = slot(arrived, unit, half), slot(arrived, unit, 2 + half)

            def add(at, mine=mine, out=out, one=one, two=two):
                g = (mine[at].astype(F32) + one[at].astype(F32) + two[at].astype(F32)).astype(BF16)
                out[at] = g
                wide = g.astype(F32)
                wide = wide * wide
                total = wide[:, :LANES]
                for k in range(1, wide.shape[1] // LANES):
                    total = total + wide[:, k * LANES : (k + 1) * LANES]
                squares[n] = squares[n] + total

            each(unit, add)

    firsts = {True: (dyt_ref, dht_ref), False: (a1t_ref, a0t_ref)}
    seconds = {True: (hid1_ref, hid0_ref), False: (dgu1_ref, dgu0_ref)}
    loads = []
    for k, ref in enumerate((dyt_ref, a1t_ref, dht_ref, a0t_ref)):
        loads.append(pltpu.make_async_copy(ref, lefts.at[k], left_sem.at[k]))

    def chunks(u):
        down, _, start_, size = units[u]
        scale = 1 if down else 2
        return scale * start_, scale * size, -(-scale * size // CHUNK)

    def source(u):
        down, layer, _, _ = units[u]
        return seconds[down][layers - 1 - layer]

    def fetch(u, c, parity):
        base, width, _ = chunks(u)
        first = base + jnp.minimum(c * CHUNK, width - CHUNK)
        return pltpu.make_async_copy(source(u).at[:, pl.ds(pl.multiple_of(first, LANES), CHUNK)], rights.at[parity], right_sem.at[parity])

    fetch(0, 0, 0).start()
    loads[0].start()
    for load in loads[1:]:
        load.start()

    done = 0
    for u, unit in enumerate(units):
        down, layer, begin, size = unit
        which = 2 * (layers - 1 - layer) + (0 if down else 1)
        base, width, count = chunks(u)
        if begin == 0:
            loads[which].wait()

        def one(c, _, u=u, down=down, layer=layer, which=which, base=base, width=width, count=count, done=done):
            parity = lax.rem(done + c, 2)
            fetch(u, c, parity).wait()

            @pl.when(c + 1 < count)
            def _():
                fetch(u, c + 1, 1 - parity).start()

            if u + 1 < len(units):
                @pl.when(c + 1 == count)
                def _():
                    fetch(u + 1, 0, 1 - parity).start()

            g = jnp.dot(lefts[which], rights[parity], preferred_element_type=F32).astype(BF16)
            first = base + jnp.minimum(c * CHUNK, width - CHUNK)
            if down:
                own_d[layer, pl.ds(pl.multiple_of(first, LANES), CHUNK), :] = g.T
            else:
                at = pl.ds(pl.multiple_of(first // 2, LANES), LANES)
                own_gu[layer, 0, :, at] = g[:, :LANES]
                own_gu[layer, 1, :, at] = g[:, LANES:]
            return 0

        lax.fori_loop(0, count, one, 0)
        done += count
        if u == 0:
            squares[n] = jnp.zeros(squares.shape[1:], F32)
            pl.semaphore_wait(barrier, n - 1)
        start(u, VIA_LEFT, VIA_RIGHT, OWN_LEFT, OWN_RIGHT)
        if u >= 1:
            forward_sums(u - 1)
        if u >= 2:
            finish(u - 2)
    last = len(units) - 1
    start(0, ALL_LEFT, ALL_RIGHT)
    forward_sums(last)
    finish(last - 1)
    finish(last)

    squares[me] = squares[n]
    exchange = [
        pltpu.make_async_remote_copy(src_ref=squares.at[me], dst_ref=squares.at[me], send_sem=sq_send.at[step], recv_sem=sq_recv.at[step],
                                     device_id={"dp": lax.rem(me + step, n)}, device_id_type=MESH)
        for step in range(1, n)
    ]
    for copy in exchange:
        copy.start()
    for u in range(1, len(units)):
        start(u, ALL_LEFT, ALL_RIGHT)
    for copy in exchange:
        copy.wait_recv()
    total = squares[0]
    for k in range(1, n):
        total = total + squares[k]
    sq_out[...] = total

    for u in range(len(units)):
        arrive(u, ALL_LEFT, ALL_RIGHT)
        start(u, FAR_LEFT, FAR_RIGHT)
    outs = []
    for u, (down, layer, begin, size) in enumerate(units):
        arrive(u, FAR_LEFT, FAR_RIGHT)
        at = pl.ds(begin, size)
        if down:
            outs.append(pltpu.make_async_copy(all_d.at[layer, at, :], gd_out.at[layer, at, :], out_sem.at[u, 0]))
            outs[-1].start()
        else:
            for k, out in enumerate((gg_out, gu_out)):
                outs.append(pltpu.make_async_copy(all_gu.at[layer, k, :, at], out.at[layer, :, at], out_sem.at[u, k]))
                outs[-1].start()
    for u in range(len(units)):
        for kind in range(10):
            remote(u, kind).wait_send()
    for copy in exchange:
        copy.wait_send()
    for out in outs:
        out.wait()


def reduced(n, layers, d, ff, tokens, parts):
    hbm = pl.BlockSpec(memory_space=pl.ANY)
    units = len(units_of(layers, ff))
    dma = pltpu.SemaphoreType.DMA
    return pl.pallas_call(
        functools.partial(reduce_kernel, n),
        out_shape=[
            jax.ShapeDtypeStruct((layers, ff, d), BF16),
            jax.ShapeDtypeStruct((layers, d, ff), BF16),
            jax.ShapeDtypeStruct((layers, d, ff), BF16),
            jax.ShapeDtypeStruct((16, LANES), F32),
        ],
        in_specs=[hbm] * 8,
        out_specs=[hbm] * 3 + [pl.BlockSpec(memory_space=pltpu.VMEM)],
        scratch_shapes=[
            pltpu.VMEM((4, d, tokens), BF16),
            pltpu.VMEM((2, tokens, CHUNK), BF16),
            pltpu.VMEM((layers, ff, d), BF16),
            pltpu.VMEM((layers, 2, d, ff), BF16),
            pltpu.VMEM((2, layers, ff // (2 * n), d), BF16),
            pltpu.VMEM((2, layers, 2, d // (2 * n), ff), BF16),
            pltpu.VMEM((4, layers, ff // (2 * n), d), BF16),
            pltpu.VMEM((4, layers, 2, d // (2 * n), ff), BF16),
            pltpu.VMEM((layers, ff, d), BF16),
            pltpu.VMEM((layers, 2, d, ff), BF16),
            pltpu.VMEM((n + 1, 16, LANES), F32),
            dma((4,)),
            dma((2,)),
            dma((units, 10)),
            dma((units, 10)),
            dma((n,)),
            dma((n,)),
            dma((units, 2)),
        ],
        compiler_params=pltpu.CompilerParams(vmem_limit_bytes=VMEM_LIMIT, collective_id=0, has_side_effects=True),
        cost_estimate=pl.CostEstimate(flops=2 * 6 * tokens * d * ff, bytes_accessed=16 * tokens * ff, transcendentals=0),
        name="reduce",
    )(*parts)


def adamw_kernel(count, sq_ref, *refs):
    factor = jnp.minimum(1.0, 0.5 * lax.rsqrt(jnp.sum(sq_ref[...], keepdims=True) / count + 1e-30))
    for i in range(3):
        g_ref, w_ref, m_ref, v_ref, new_w, new_m, new_v = refs[i::3]
        g = g_ref[...].astype(F32) * factor
        w = w_ref[...].astype(F32)
        m = 0.9 * m_ref[...] + 0.1 * g
        v = 0.95 * v_ref[...] + 0.05 * g * g
        step = m * lax.rsqrt(v + 1e-8) + 0.1 * w
        new_w[...] = (w - 0.02 * step).astype(BF16)
        new_m[...] = m
        new_v[...] = v


def adamw(squares, gradients, weights, m, v, steps=16):
    flat = [[a.reshape(-1, a.shape[-1]) for a in group] for group in (gradients, weights, m, v)]
    shapes = [w.shape for w in flat[1]]
    specs = [pl.BlockSpec((rows // steps, columns), lambda i: (i, 0)) for rows, columns in shapes]
    count = sum(w.size for w in weights)
    new = pl.pallas_call(
        functools.partial(adamw_kernel, count),
        grid=(steps,),
        out_shape=[jax.ShapeDtypeStruct(shape, dtype) for dtype in (BF16, F32, F32) for shape in shapes],
        in_specs=[pl.BlockSpec(squares.shape, lambda i: (0, 0))] + specs * 4,
        out_specs=specs * 3,
        compiler_params=pltpu.CompilerParams(vmem_limit_bytes=VMEM_LIMIT, dimension_semantics=("arbitrary",)),
        cost_estimate=pl.CostEstimate(flops=16 * count, bytes_accessed=22 * count, transcendentals=count),
        name="adamw",
    )(squares, *(a for group in flat for a in group))
    return tuple(a.reshape(w.shape) for a, w in zip(new, weights * 3, strict=True))


def solution(mesh):
    n = mesh.shape["dp"]

    def step(x, dy, *arrays):
        weights, m, v = (arrays[i : i + 3] for i in (0, 3, 6))
        layers, ff, d = weights[2].shape
        parts = tokens_pass(x, dy, *weights)
        gd, gg, gu, squares = reduced(n, layers, d, ff, x.shape[1], parts)
        return adamw(squares, (gg, gu, gd), weights, m, v)

    return jax.shard_map(
        step,
        mesh=mesh,
        in_specs=(P(("rep", "dp"), None, None),) * 2 + (P(None, None, None),) * 9,
        out_specs=(P("rep", None, None),) * 9,
        check_vma=False,
    )
```

time: 547 us -> 323 us (0.59); the launches traced: 539 us -> 322 us
  Pallas kernels: 0 us -> 321 us
  matrix products: 269 us -> 0 us
  waiting for transfers between devices: 185 us -> 0 us
  other arithmetic: 53 us -> 0 us
  local copies, waits for them, and re-layouts: 15.9 us -> 0 us
  between operations: 16.7 us -> 0.82 us
    pallas_call x0 -> x3, Pallas kernels: none -> 321 us  [the longest x1 194 us: reduced(): pl.pallas_call(functools.partial(reduce_kernel, n), out_shape=[jax.ShapeD...]
    dot_general x15 -> x0, matrix products: 269 us -> none  [the longest x5 101 us: layer(): gate = jnp.dot(a, w['w_gate'], preferred_element_type=jnp.float32)]
    psum x1 -> x0, waiting for transfers between devices: 185 us -> none  [step(): summed[number] = [lax.psum(by_w[name], 'dp') for name in NAMES]]
    convert_element_type x2 -> x0, other arithmetic: 35.5 us -> none  [adamw(): return ((w - 0.02 * step).astype(jnp.bfloat16), m, v)]
    unnamed x44 -> x0, local copies, waits for them, and re-layouts: 15.9 us -> none
    reduce_sum x4 -> x0, other arithmetic: 14.4 us -> none  [the longest x3 11.1 us: step(): jnp.sum(g * g)]
  transfers between devices with their start and end apart: 1 -> 0, of which waited for: 1 -> 0; matrix products, arithmetic and copies ran while one was open for 0% -> 0% of each run, Pallas kernels for 0% -> 0%
where the time goes in v1:
time: 323 us; the launch traced here: 322 us
  Pallas kernels  321 us (99%)
    pallas_call x1, Pallas kernels, reduced(): pl.pallas_call(functools.partial(reduce_kernel, n), out_shape=[jax.ShapeD...  194 us
    pallas_call x1, Pallas kernels, tokens_pass(): pl.pallas_call(functools.partial(tokens_kernel, many=2), grid=(tokens //...  85.7 us
    pallas_call x1, Pallas kernels, adamw(): pl.pallas_call(functools.partial(adamw_kernel, count), grid=(steps,), out...  41.3 us

profile of v1, /device:TPU:112, one launch (start us, length us, event | category | flops | bytes accessed | tf_op | source)
XLA Modules:
  0.0 321.7 jit_solution(345153576992856946)
XLA Ops:
  0.6 85.7 %tokens.1 = (bf16[512,4096]{1,0:T(8,128)(2,1)}, bf16[512,4096]{1,0:T(8,128)(2,1)}, bf16[512,4096]{1,0:T(8,128)(2,1)}, bf16[512,4096]{1,0:T(8,128)(2,1)}, bf16[40...) custom-call(bf16[1,4096,512]{2,1,0:T(8,128)(2,1)} %x_ref.1, ...), custom_call_target="tpu_custom_call" | custom-call | flops 62813896704 | bytes 109051904 | tf_op jit(solution)/shard_map/tokens/pallas_call | solution.py:100
  86.4 193.8 %reduce.1 = (bf16[2,1664,512]{2,1,0:T(8,128)(2,1)}, bf16[2,512,1664]{2,1,0:T(8,128)(2,1)}, bf16[2,512,1664]{2,1,0:T(8,128)(2,1)}, f32[16,128]{1,0:T(8,128)}) custom-call(bf16[512,4096]{1,0:T(8,128)(2,1)} %get-tuple-element.30.dyt_ref, bf16[512,4096]{1,0:T(8,128)(2,1)} %get-tuple-element.31.a1t_ref, bf16[512,4096]{1,0:T(8,128)(2,1)} %get-tuple-element.32.dht_ref, ...), custom_call_target="tpu_custom_call" | custom-call | flops 41875931136 | bytes 109051904 | tf_op jit(solution)/shard_map/reduce/pallas_call | solution.py:339
  280.2 41.3 %adamw.1 = (bf16[1024,1664]{1,0:T(8,128)(2,1)}, bf16[1024,1664]{1,0:T(8,128)(2,1)}, bf16[3328,512]{1,0:T(8,128)(2,1)}, f32[1024,1664]{1,0:T(8,128)}, f32[1024,16...) custom-call(f32[16,128]{1,0:T(8,128)} %get-tuple-element.38.sq_ref, ...), custom_call_target="tpu_custom_call" | custom-call | flops 81788928 | bytes 112459776 | tf_op jit(solution)/shard_map/adamw/pallas_call | solution.py:394

commit v2 on v1

v2 whole, which is shorter than its diff:
```python
import functools

import jax
import jax.numpy as jnp
from jax import lax
from jax.experimental import pallas as pl
from jax.experimental.pallas import tpu as pltpu
from jax.sharding import PartitionSpec as P

F32, BF16 = jnp.float32, jnp.bfloat16
MESH = pl.DeviceIdType.MESH
LANES = 128
VMEM_LIMIT = 67043328
TILE = 512
CHUNK = 4 * LANES


def by_columns(a, b):
    return lax.dot_general(a, b, (((1,), (1,)), ((), ())), preferred_element_type=F32)


def scaled(h):
    wide = h.astype(F32)
    scale = lax.rsqrt(jnp.mean(wide * wide, -1, keepdims=True) + 1e-6)
    return wide, scale, (wide * scale).astype(BF16)


def lane(k):
    return pl.ds(k * LANES, LANES)


def side_by_side(wg_ref, wu_ref, wgu, n, sems):
    return [
        pltpu.make_async_copy(ref.at[n, :, lane(k)], wgu.at[:, lane(2 * k + which)], sems.at[2 * k + which])
        for k in range(wg_ref.shape[-1] // LANES)
        for which, ref in enumerate((wg_ref, wu_ref))
    ]


def grouped(blocks, many):
    return [(k, min(many, blocks - k)) for k in range(0, blocks, many)]


def tokens_kernel(x_ref, dy_ref, wg_ref, wu_ref, wd_ref, dyt_ref, a1t_ref, a0t_ref, h1_ref, hid1_ref, dgu1_ref, hid0_ref,
                  keep_ref, wgu, wd, sems, *, many):
    layers, ff, _ = wd.shape
    blocks = ff // LANES

    @pl.when(pl.program_id(0) == 0)
    def _():
        copies = []
        for n in range(layers):
            copies += side_by_side(wg_ref, wu_ref, wgu.at[n], n, sems.at[n])
            copies.append(pltpu.make_async_copy(wd_ref.at[n], wd.at[n], sems.at[n, 2 * blocks]))
        for copy in copies:
            copy.start()
        for copy in copies:
            copy.wait()

    groups = grouped(blocks, many)
    h0 = x_ref[...]
    _, _, a0 = scaled(h0)
    a0t_ref[...] = a0.T
    for k, count in groups:
        gu = jnp.dot(a0, wgu[0, :, pl.ds(2 * k * LANES, 2 * count * LANES)], preferred_element_type=F32)
        for i in range(count):
            g, u = (gu[:, (2 * i + j) * LANES : (2 * i + j + 1) * LANES] for j in range(2))
            s = 0.5 * jnp.tanh(0.5 * g) + 0.5
            silu = g * s
            hid0_ref[:, lane(k + i)] = (silu * u).astype(BF16)
            keep_ref[:, lane(2 * (k + i))] = (s + silu * (1.0 - s)) * u
            keep_ref[:, lane(2 * (k + i) + 1)] = silu
    h1 = h0 + jnp.dot(hid0_ref[...], wd[0], preferred_element_type=F32).astype(BF16)
    h1_ref[...] = h1
    _, _, a1 = scaled(h1)
    a1t_ref[...] = a1.T
    dy = dy_ref[...]
    dyt_ref[...] = dy.T
    for k, count in groups:
        gu = jnp.dot(a1, wgu[1, :, pl.ds(2 * k * LANES, 2 * count * LANES)], preferred_element_type=F32)
        dhid = by_columns(dy, wd[1, pl.ds(k * LANES, count * LANES), :]).astype(BF16).astype(F32)
        for i in range(count):
            g, u = (gu[:, (2 * i + j) * LANES : (2 * i + j + 1) * LANES] for j in range(2))
            dh = dhid[:, i * LANES : (i + 1) * LANES]
            s = 0.5 * jnp.tanh(0.5 * g) + 0.5
            silu = g * s
            hid1_ref[:, lane(k + i)] = (silu * u).astype(BF16)
            dgu1_ref[:, lane(2 * (k + i))] = (dh * u * (s + silu * (1.0 - s))).astype(BF16)
            dgu1_ref[:, lane(2 * (k + i) + 1)] = (dh * silu).astype(BF16)


def tokens_pass(x, dy, wg, wu, wd):
    _, tokens, d = x.shape
    layers, ff, _ = wd.shape
    tile = min(TILE, tokens)
    lead = pl.BlockSpec((None, tile, d), lambda i: (0, i, 0))
    hbm = pl.BlockSpec(memory_space=pl.ANY)
    turned = pl.BlockSpec((d, tile), lambda i: (0, i))
    widths = (d, ff, 2 * ff, ff, 2 * ff)
    return pl.pallas_call(
        functools.partial(tokens_kernel, many=2),
        grid=(tokens // tile,),
        out_shape=[jax.ShapeDtypeStruct((d, tokens), BF16)] * 3 + [
            jax.ShapeDtypeStruct((tokens, n), F32 if k == 4 else BF16) for k, n in enumerate(widths)
        ],
        in_specs=[lead, lead, hbm, hbm, hbm],
        out_specs=[turned] * 3 + [pl.BlockSpec((tile, n), lambda i: (i, 0)) for n in widths],
        scratch_shapes=[
            pltpu.VMEM((layers, d, 2 * ff), BF16),
            pltpu.VMEM((layers, ff, d), BF16),
            pltpu.SemaphoreType.DMA((layers, 2 * ff // LANES + 1)),
        ],
        compiler_params=pltpu.CompilerParams(vmem_limit_bytes=VMEM_LIMIT, dimension_semantics=("arbitrary",)),
        cost_estimate=pl.CostEstimate(flops=2 * 6 * tokens * d * ff, bytes_accessed=10 * tokens * ff, transcendentals=2 * tokens * ff),
        name="tokens",
    )(x, dy, wg, wu, wd)


(VIA_LEFT, VIA_RIGHT, OWN_LEFT, OWN_RIGHT, SUM_LEFT, SUM_RIGHT, ALL_LEFT, ALL_RIGHT, FAR_LEFT, FAR_RIGHT) = range(10)


def units_of(layers, ff):
    cuts = {True: CHUNK, False: (ff // CHUNK) * CHUNK // 2}
    return [
        (down, n, start, size)
        for n in reversed(range(layers))
        for down, cut in cuts.items()
        for start, size in ((0, cut), (cut, ff - cut))
    ]


def reduce_kernel(n, dyt_ref, a1t_ref, a0t_ref, h1_ref, hid1_ref, dgu1_ref, hid0_ref, keep_ref, dy_ref, wg_ref, wu_ref, wd_ref,
                  gd_out, gg_out, gu_out, part_a, part_b, sq_out, places, dgu0_ref,
                  lefts, rights, own_d, own_gu, via_d, via_gu, in_d, in_gu, all_d, all_gu, mine_d, mine_gu, squares,
                  wgu, wd, dgu1_in, keep_in, small_in, dgu0_tile,
                  left_sem, right_sem, send, recv, sq_send, sq_recv, out_sem, weight_sem, tile_sem, back_sem):
    layers, ff, d = own_d.shape
    tile = dgu0_tile.shape[1]
    tiles = h1_ref.shape[0] // tile
    units = units_of(layers, ff)
    me = lax.axis_index("dp")
    right, left, far = lax.rem(me + 1, n), lax.rem(me + n - 1, n), lax.rem(me + n // 2, n)

    barrier = pltpu.get_barrier_semaphore()
    for step in range(1, n):
        pl.semaphore_signal(barrier, inc=1, device_id={"dp": lax.rem(me + step, n)}, device_id_type=MESH)

    def within(unit, owner, half):
        down, _, start, size = unit
        if down:
            rows = pl.ds(start, size) if half is None else pl.ds(start + half * (size // 2), size // 2)
            return rows, pl.ds(pl.multiple_of(owner * LANES, LANES), LANES)
        rows = d // n
        first = owner * rows
        if half is not None:
            rows = rows // 2
            first = first + half * rows
        return slice(None), pl.ds(pl.multiple_of(first, 16), rows), pl.ds(start, size)

    def share(ref, unit, owner, half):
        return ref[0 if unit[0] else 1].at[(unit[1], *within(unit, owner, half))]

    def shared(unit, owner, half):
        return whole[0 if unit[0] else 1].at[within(unit, owner, half)]

    def slot(ref, unit, k):
        down, layer, start, size = unit
        if down:
            return ref[0].at[k, pl.ds(start // 2, size // 2), :]
        return ref[1].at[k, :, :, pl.ds(start, size)]

    def summed(unit, half):
        if unit[1]:
            return shared(unit, me, half)
        return (mine_d if unit[0] else mine_gu).at[within(unit, 0, half)]

    own, via, arrived, whole = (own_d, own_gu), (via_d, via_gu), (in_d, in_gu), (all_d, all_gu)

    def remote(u, kind):
        unit = units[u]
        to = left if kind % 2 == 0 else right
        if kind in (VIA_LEFT, VIA_RIGHT):
            src, dst = share(own, unit, far, kind - VIA_LEFT), slot(via, unit, kind - VIA_LEFT)
        elif kind in (OWN_LEFT, OWN_RIGHT):
            src, dst = share(own, unit, to, 1 if kind == OWN_LEFT else 0), slot(arrived, unit, 1 if kind == OWN_LEFT else 0)
        elif kind in (SUM_LEFT, SUM_RIGHT):
            src, dst = share(own, unit, to, kind - SUM_LEFT), slot(arrived, unit, 2 + kind - SUM_LEFT)
        elif kind in (ALL_LEFT, ALL_RIGHT):
            src = dst = shared(unit, me, None)
        else:
            src = dst = shared(unit, right if kind == FAR_LEFT else left, 1 if kind == FAR_LEFT else 0)
        return pltpu.make_async_remote_copy(src_ref=src, dst_ref=dst, send_sem=send.at[u, kind], recv_sem=recv.at[u, kind],
                                            device_id={"dp": to}, device_id_type=MESH)

    def start(u, *kinds):
        for kind in kinds:
            remote(u, kind).start()

    def arrive(u, *kinds):
        for kind in kinds:
            remote(u, kind).wait_recv()

    def each(unit, body):
        down, _, _, size = unit
        many = 64 if down else 16
        blocks = (size // 2 if down else d // (2 * n)) // many
        for which in range(1 if down else 2):
            def one(i, _, which=which):
                rows = pl.ds(pl.multiple_of(i * many, many), many)
                body((rows, slice(None)) if down else (which, rows, slice(None)))
                return 0

            lax.fori_loop(0, blocks, one, 0)

    def forward_sums(u):
        unit = units[u]
        for k, kind, owner in ((0, SUM_LEFT, left), (1, SUM_RIGHT, right)):
            arrive(u, VIA_LEFT + k)
            mine, other = share(own, unit, owner, k), slot(via, unit, k)

            def add(at, mine=mine, other=other):
                mine[at] = (mine[at].astype(F32) + other[at].astype(F32)).astype(BF16)

            each(unit, add)
            start(u, kind)

    def finish(u):
        unit = units[u]
        arrive(u, OWN_LEFT, OWN_RIGHT, SUM_LEFT, SUM_RIGHT)
        for half in range(2):
            mine, out = share(own, unit, me, half), summed(unit, half)
            one, two = slot(arrived, unit, half), slot(arrived, unit, 2 + half)

            def add(at, mine=mine, out=out, one=one, two=two):
                g = (mine[at].astype(F32) + one[at].astype(F32) + two[at].astype(F32)).astype(BF16)
                out[at] = g
                wide = g.astype(F32)
                wide = wide * wide
                total = wide[:, :LANES]
                for k in range(1, wide.shape[1] // LANES):
                    total = total + wide[:, k * LANES : (k + 1) * LANES]
                squares[n] = squares[n] + sum(total[16 * k : 16 * (k + 1)] for k in range(total.shape[0] // 16))

            each(unit, add)

    seconds = {True: (hid1_ref, hid0_ref), False: (dgu1_ref, dgu0_ref)}
    loads = {
        (True, layers - 1): pltpu.make_async_copy(dyt_ref, lefts.at[0], left_sem.at[0]),
        (False, layers - 1): pltpu.make_async_copy(a1t_ref, lefts.at[1], left_sem.at[1]),
        (False, 0): pltpu.make_async_copy(a0t_ref, lefts.at[1], left_sem.at[2]),
    }

    def chunks(u):
        down, _, start_, size = units[u]
        scale = 1 if down else 2
        return scale * start_, scale * size, -(-scale * size // CHUNK)

    def source(u):
        down, layer, _, _ = units[u]
        return seconds[down][layers - 1 - layer]

    def fetch(u, c, parity):
        base, width, _ = chunks(u)
        first = base + jnp.minimum(c * CHUNK, width - CHUNK)
        return pltpu.make_async_copy(source(u).at[:, pl.ds(pl.multiple_of(first, LANES), CHUNK)], rights.at[parity], right_sem.at[parity])

    blocks = ff // LANES
    weight_loads = side_by_side(wg_ref, wu_ref, wgu, layers - 1, weight_sem.at[0])
    weight_loads.append(pltpu.make_async_copy(wd_ref.at[0], wd, weight_sem.at[0, 2 * blocks]))

    def tile_loads(i, parity):
        rows = pl.ds(pl.multiple_of(i * tile, tile), tile)
        copies = [pltpu.make_async_copy(dgu1_ref.at[rows, :], dgu1_in.at[parity], tile_sem.at[0, parity])]
        copies.append(pltpu.make_async_copy(keep_ref.at[rows, :], keep_in.at[parity], tile_sem.at[1, parity]))
        for k, ref in enumerate((h1_ref.at[rows, :], dy_ref.at[0, rows, :])):
            copies.append(pltpu.make_async_copy(ref, small_in.at[k, parity], tile_sem.at[2 + k, parity]))
        return copies

    def tile_store(i, parity):
        rows = pl.ds(pl.multiple_of(i * tile, tile), tile)
        return pltpu.make_async_copy(dgu0_tile.at[parity], dgu0_ref.at[rows, :], back_sem.at[parity])

    def one_tile(i):
        parity = lax.rem(i, 2)
        for copy in tile_loads(i, parity):
            copy.wait()

        @pl.when(i + 1 < tiles)
        def _():
            for copy in tile_loads(i + 1, 1 - parity):
                copy.start()

        @pl.when(i >= 2)
        def _():
            tile_store(i - 2, parity).wait()

        wide, scale, _ = scaled(small_in[0, parity])
        da = by_columns(dgu1_in[parity], wgu[...]).astype(BF16).astype(F32)
        along = jnp.mean(da * wide, -1, keepdims=True)
        dh1 = small_in[1, parity] + (scale * (da - wide * (scale * scale) * along)).astype(BF16)
        lefts[0, :, pl.ds(pl.multiple_of(i * tile, tile), tile)] = dh1.T
        for k, count in grouped(blocks, 4):
            dhid = by_columns(dh1, wd[pl.ds(k * LANES, count * LANES), :]).astype(BF16).astype(F32)
            for j in range(count):
                dh = dhid[:, j * LANES : (j + 1) * LANES]
                for which in range(2):
                    at = lane(2 * (k + j) + which)
                    dgu0_tile[parity, :, at] = (dh * keep_in[parity, :, at]).astype(BF16)
        tile_store(i, parity).start()

    def hand_on(u):
        arrive(u, ALL_LEFT, ALL_RIGHT)
        start(u, FAR_LEFT, FAR_RIGHT)

    def finish_and_send(u):
        finish(u)
        start(u, ALL_LEFT, ALL_RIGHT)

    def tokens_backward(half):
        beside = {1: [(hand_on, 0)], 3: [(forward_sums, half - 1)], 7: [(hand_on, 1)], 10: [(finish_and_send, half - 2)],
                  13: [(finish_and_send, half - 1)]}
        for copy in weight_loads:
            copy.wait()
        loads[(False, 0)].start()

        def one(i, _):
            one_tile(i)
            for when, actions in beside.items():
                @pl.when(i == min(when, tiles - 1))
                def _(actions=actions):
                    for action, u in actions:
                        action(u)
            return 0

        lax.fori_loop(0, tiles, one, 0)
        for i in range(max(0, tiles - 2), tiles):
            tile_store(i, i % 2).wait()

    fetch(0, 0, 0).start()
    loads[(True, layers - 1)].start()
    loads[(False, layers - 1)].start()
    for copy in weight_loads + tile_loads(0, 0):
        copy.start()

    done = 0
    half = len(units) // layers
    for u, unit in enumerate(units):
        down, layer, begin, size = unit
        which = 0 if down else 1
        base, width, count = chunks(u)
        if u == half:
            tokens_backward(half)
            fetch(u, 0, done % 2).start()
        if begin == 0 and (down, layer) in loads:
            loads[(down, layer)].wait()

        def one(c, _, u=u, down=down, layer=layer, which=which, base=base, width=width, count=count, done=done):
            parity = lax.rem(done + c, 2)
            fetch(u, c, parity).wait()

            @pl.when(c + 1 < count)
            def _():
                fetch(u, c + 1, 1 - parity).start()

            if u + 1 < len(units) and u + 1 != half:
                @pl.when(c + 1 == count)
                def _():
                    fetch(u + 1, 0, 1 - parity).start()

            g = jnp.dot(lefts[which], rights[parity], preferred_element_type=F32).astype(BF16)
            first = base + jnp.minimum(c * CHUNK, width - CHUNK)
            if down:
                own_d[layer, pl.ds(pl.multiple_of(first, LANES), CHUNK), :] = g.T
            else:
                for k in range(CHUNK // LANES):
                    at = pl.ds(pl.multiple_of(first // 2 + k // 2 * LANES, LANES), LANES)
                    own_gu[layer, k % 2, :, at] = g[:, k * LANES : (k + 1) * LANES]
            if u % half:
                @pl.when(c == max(0, count - 2))
                def _():
                    forward_sums(u - 1)
            return 0

        lax.fori_loop(0, count, one, 0)
        done += count
        if u == 0:
            squares[n] = jnp.zeros(squares.shape[1:], F32)
            pl.semaphore_wait(barrier, n - 1)
        start(u, VIA_LEFT, VIA_RIGHT, OWN_LEFT, OWN_RIGHT)
        place = u % half
        if u in (half, half + 1):
            hand_on(u - 2)
        if place >= 2:
            finish(u - 2)
            if u < half:
                start(u - 2, ALL_LEFT, ALL_RIGHT)
        if u == half + 2:
            for k in range(half):
                arrive(k, FAR_LEFT, FAR_RIGHT)
            outs = [pltpu.make_async_copy(all_d, gd_out, out_sem.at[0])]
            for k, out in enumerate((gg_out, gu_out)):
                outs.append(pltpu.make_async_copy(all_gu.at[k], out, out_sem.at[1 + k]))
            for out in outs:
                out.start()
    last = len(units) - 1
    parts = []
    many = d // (2 * n)
    for k, part in enumerate((part_a, part_b)):
        for block in range(blocks):
            rows = pl.ds(k * (ff // 2) + block * many, many)
            parts.append(pltpu.make_async_copy(mine_d.at[rows, :], part.at[2, :, lane(block)], out_sem.at[3 + k * (blocks + 1) + block]))
    for part in parts:
        part.start()
    forward_sums(last)
    finish(last - 1)
    finish(last)

    squares[me] = squares[n]
    exchange = [
        pltpu.make_async_remote_copy(src_ref=squares.at[me], dst_ref=squares.at[me], send_sem=sq_send.at[step], recv_sem=sq_recv.at[step],
                                     device_id={"dp": lax.rem(me + step, n)}, device_id_type=MESH)
        for step in range(1, n)
    ]
    for copy in exchange:
        copy.start()
    for k, part in enumerate((part_a, part_b)):
        parts.append(pltpu.make_async_copy(
            mine_gu.at[:, pl.ds(k * many, many), :], part.at[pl.ds(0, 2)], out_sem.at[3 + k * (blocks + 1) + blocks]))
        parts[-1].start()
    for k, (owner, side) in enumerate(((me, 0), (me, 1), (left, 0), (right, 1), (left, 1), (right, 0), (far, 0), (far, 1))):
        places[k] = 2 * owner + side
    for copy in exchange:
        copy.wait_recv()
    total = squares[0]
    for k in range(1, n):
        total = total + squares[k]
    sq_out[...] = total
    for u in range(len(units)):
        for kind in range(10 if u < half else ALL_LEFT):
            remote(u, kind).wait_send()
    for copy in exchange:
        copy.wait_send()
    for out in outs + parts:
        out.wait()


def reduced(n, layers, d, ff, tokens, parts, dy, weights):
    hbm = pl.BlockSpec(memory_space=pl.ANY)
    units = len(units_of(layers, ff))
    tile = min(TILE // 2, tokens)
    dma = pltpu.SemaphoreType.DMA
    part = jax.ShapeDtypeStruct((3, d // (2 * n), ff), BF16)
    return pl.pallas_call(
        functools.partial(reduce_kernel, n),
        out_shape=[
            jax.ShapeDtypeStruct((ff, d), BF16),
            jax.ShapeDtypeStruct((d, ff), BF16),
            jax.ShapeDtypeStruct((d, ff), BF16),
            part,
            part,
            jax.ShapeDtypeStruct((16, LANES), F32),
            jax.ShapeDtypeStruct((2 * n,), jnp.int32),
            jax.ShapeDtypeStruct((tokens, 2 * ff), BF16),
        ],
        in_specs=[hbm] * 12,
        out_specs=[hbm] * 5 + [pl.BlockSpec(memory_space=pltpu.VMEM), pl.BlockSpec(memory_space=pltpu.SMEM), hbm],
        scratch_shapes=[
            pltpu.VMEM((2, d, tokens), BF16),
            pltpu.VMEM((2, tokens, CHUNK), BF16),
            pltpu.VMEM((layers, ff, d), BF16),
            pltpu.VMEM((layers, 2, d, ff), BF16),
            pltpu.VMEM((2, ff // 2, LANES), BF16),
            pltpu.VMEM((2, 2, d // (2 * n), ff), BF16),
            pltpu.VMEM((4, ff // 2, LANES), BF16),
            pltpu.VMEM((4, 2, d // (2 * n), ff), BF16),
            pltpu.VMEM((ff, d), BF16),
            pltpu.VMEM((2, d, ff), BF16),
            pltpu.VMEM((ff, LANES), BF16),
            pltpu.VMEM((2, d // n, ff), BF16),
            pltpu.VMEM((n + 1, 16, LANES), F32),
            pltpu.VMEM((d, 2 * ff), BF16),
            pltpu.VMEM((ff, d), BF16),
            pltpu.VMEM((2, tile, 2 * ff), BF16),
            pltpu.VMEM((2, tile, 2 * ff), F32),
            pltpu.VMEM((2, 2, tile, d), BF16),
            pltpu.VMEM((2, tile, 2 * ff), BF16),
            dma((3,)),
            dma((2,)),
            dma((units, 10)),
            dma((units, 10)),
            dma((n,)),
            dma((n,)),
            dma((3 + 2 * (ff // LANES + 1),)),
            dma((1, 2 * ff // LANES + 1)),
            dma((4, 2)),
            dma((2,)),
        ],
        compiler_params=pltpu.CompilerParams(vmem_limit_bytes=VMEM_LIMIT, collective_id=0, has_side_effects=True),
        cost_estimate=pl.CostEstimate(flops=2 * 9 * tokens * d * ff, bytes_accessed=20 * tokens * ff, transcendentals=tokens * ff),
        name="reduce",
    )(*parts, dy, *weights)


def clip_of(sq_ref, count):
    return jnp.minimum(1.0, 0.5 * lax.rsqrt(jnp.sum(sq_ref[...], keepdims=True) / count + 1e-30))


def update(factor, g, old, new, at):
    w_ref, m_ref, v_ref = old
    g = g.astype(F32) * factor
    w = w_ref[at].astype(F32)
    m = 0.9 * m_ref[at] + 0.1 * g
    v = 0.95 * v_ref[at] + 0.05 * g * g
    step = m * lax.rsqrt(v + 1e-8) + 0.1 * w
    new[0][at] = (w - 0.02 * step).astype(BF16)
    new[1][at] = m
    new[2][at] = v


def whole_kernel(count, sq_ref, *refs):
    factor = clip_of(sq_ref, count)
    for i in range(3):
        g_ref, *old_and_new = refs[i::3]
        update(factor, g_ref[...], old_and_new[:3], old_and_new[3:], (slice(None), slice(None)))


def parts_kernel(count, many, places_ref, sq_ref, *refs):
    parts, refs = refs[:many], refs[many:]
    old, new = refs[:9], refs[18:]
    factor = clip_of(sq_ref, count)
    rows = parts[0].shape[1]
    for k, part in enumerate(parts):
        @pl.when(pl.program_id(0) == k)
        def _(part=part):
            def some(i, _):
                at = pl.ds(pl.multiple_of(i * 16, 16), 16)
                for which in range(2):
                    update(factor, part[which, at, :], old[which::3], new[which::3], (at, slice(None)))
                return 0

            lax.fori_loop(0, rows // 16, some, 0)

            for i in range(part.shape[2] // LANES):
                update(factor, part[2, :, lane(i)], old[2::3], new[2::3], (pl.ds(i * rows, rows), slice(None)))


def adamw_layer(squares, gradients, arrays, layer, blocks):
    count = sum(a.size for a in arrays[:3])
    d, ff = gradients[0].shape
    g_specs = [pl.BlockSpec((d // blocks, ff), lambda i: (i, 0))] * 2 + [pl.BlockSpec((ff // blocks, d), lambda i: (i, 0))]
    specs = [pl.BlockSpec((None, d // blocks, ff), lambda i: (layer, i, 0))] * 2 + [pl.BlockSpec((None, ff // blocks, d), lambda i: (layer, i, 0))]
    return pl.pallas_call(
        functools.partial(whole_kernel, count),
        grid=(blocks,),
        out_shape=[jax.ShapeDtypeStruct(a.shape, a.dtype) for a in arrays],
        in_specs=[pl.BlockSpec(squares.shape, lambda i: (0, 0))] + g_specs + specs * 3,
        out_specs=specs * 3,
        compiler_params=pltpu.CompilerParams(vmem_limit_bytes=VMEM_LIMIT, dimension_semantics=("arbitrary",)),
        cost_estimate=pl.CostEstimate(flops=COST * count // 2, bytes_accessed=11 * count, transcendentals=count),
        name="adamw_layer",
    )(squares, *gradients, *arrays)


def adamw_parts(squares, places, first, parts, arrays, new, layer):
    count = sum(a.size for a in arrays[:3])
    _, rows, ff = parts[0].shape
    many = len(parts)
    by_rows = pl.BlockSpec((None, rows, ff), lambda i, places: (layer, places[first + i], 0))
    by_lanes = pl.BlockSpec((None, ff // 2, LANES), lambda i, places: (layer, places[first + i] % 2, places[first + i] // 2))
    specs = [by_rows, by_rows, by_lanes]
    return pl.pallas_call(
        functools.partial(parts_kernel, count, many),
        grid_spec=pltpu.PrefetchScalarGridSpec(
            num_scalar_prefetch=1,
            grid=(many,),
            in_specs=[pl.BlockSpec(squares.shape, lambda i, places: (0, 0))]
            + [pl.BlockSpec(part.shape, lambda i, places: (0, 0, 0)) for part in parts]
            + specs * 3
            + [pl.BlockSpec(memory_space=pl.ANY)] * 9,
            out_specs=specs * 3,
        ),
        out_shape=[jax.ShapeDtypeStruct(a.shape, a.dtype) for a in arrays],
        input_output_aliases={2 + many + 9 + i: i for i in range(9)},
        compiler_params=pltpu.CompilerParams(vmem_limit_bytes=VMEM_LIMIT, dimension_semantics=("arbitrary",)),
        cost_estimate=pl.CostEstimate(flops=COST * many * 3 * rows * ff, bytes_accessed=22 * many * 3 * rows * ff, transcendentals=many * 3 * rows * ff),
        name="adamw_parts",
    )(places, squares, *parts, *arrays, *new)


COST = 200


def solution(mesh):
    n = mesh.shape["dp"]
    onward = [(i, (i + 1) % n) for i in range(n)]
    back = [(to, i) for i, to in onward]

    def step(x, dy, *arrays):
        weights = arrays[:3]
        layers, ff, d = weights[2].shape
        parts = tokens_pass(x, dy, *weights)
        gd, gg, gu, a, b, squares, places, _ = reduced(n, layers, d, ff, x.shape[1], parts, dy, weights)
        left_a, right_b = lax.ppermute(a, "dp", onward), lax.ppermute(b, "dp", back)
        left_b, right_a = lax.ppermute(b, "dp", onward), lax.ppermute(a, "dp", back)
        new = adamw_layer(squares, (gg, gu, gd), arrays, layers - 1, 4)
        left_a, right_b, *new = lax.optimization_barrier((left_a, right_b, *new))
        far_a, far_b = lax.ppermute(left_a, "dp", onward), lax.ppermute(right_b, "dp", back)
        for first, some in ((0, (a, b, left_a, right_b)), (4, (left_b, right_a, far_a, far_b))):
            new = adamw_parts(squares, places, first, some, arrays, new, 0)
        return tuple(new)

    return jax.shard_map(
        step,
        mesh=mesh,
        in_specs=(P(("rep", "dp"), None, None),) * 2 + (P(None, None, None),) * 9,
        out_specs=(P("rep", None, None),) * 9,
        check_vma=False,
    )
```

time: 323 us -> 266 us (0.82)
  Pallas kernels: 321 us -> 252 us
  starting transfers between devices: 0 us -> 8.65 us
  waiting for transfers between devices: 0 us -> 3.46 us
    pallas_call x1, Pallas kernels: 194 us -> 147 us  [reduced(): pl.pallas_call(functools.partial(reduce_kernel, n), out_shape=[jax.ShapeD...]
    pallas_call x1, Pallas kernels: 85.7 us -> 60.9 us  [tokens_pass(): pl.pallas_call(functools.partial(tokens_kernel, many=2), grid=(tokens //...]
    ppermute x0 -> x6, starting transfers between devices: none -> 8.65 us  [the longest x1 3.21 us: step(): lax.ppermute(right_b, 'dp', back)]
    ppermute x0 -> x6, waiting for transfers between devices: none -> 3.46 us  [the longest x1 3.45 us: step(): lax.ppermute(left_a, 'dp', onward)]
    pallas_call x1 -> x3, Pallas kernels: 41.3 us -> 44.6 us  [the longest x2 25.2 us: adamw_parts(): pl.pallas_call(functools.partial(parts_kernel, count, many), grid_spec=pl...]
  transfers between devices with their start and end apart: 0 -> 6, of which waited for: 0 -> 1; matrix products, arithmetic and copies ran while one was open for 0% -> 0% of each run, Pallas kernels for 0% -> 12%
where the time goes in v2:
time: 266 us; the launch traced here: 265 us
  Pallas kernels  252 us (95%)
  starting transfers between devices  8.65 us (3%)
  waiting for transfers between devices  3.46 us (1%)
    pallas_call x1, Pallas kernels, reduced(): pl.pallas_call(functools.partial(reduce_kernel, n), out_shape=[jax.ShapeD...  147 us
    pallas_call x1, Pallas kernels, tokens_pass(): pl.pallas_call(functools.partial(tokens_kernel, many=2), grid=(tokens //...  60.9 us
    pallas_call x2, Pallas kernels, adamw_parts(): pl.pallas_call(functools.partial(parts_kernel, count, many), grid_spec=pl...  25.2 us
    pallas_call x1, Pallas kernels, adamw_layer(): pl.pallas_call(functools.partial(whole_kernel, count), grid=(blocks,), ou...  19.4 us
  transfers between devices with their start and end apart: 6, of which 1 were waited for; matrix products, arithmetic and copies ran while one was open for 0% of the time, Pallas kernels for 12%

profile of v2, /device:TPU:112, one launch (start us, length us, event | category | flops | bytes accessed | tf_op | source)
XLA Modules:
  0.0 265.4 jit_solution(2901539934323895417)
XLA Ops:
  0.6 60.9 %tokens.1 = (bf16[512,4096]{1,0:T(8,128)(2,1)}, bf16[512,4096]{1,0:T(8,128)(2,1)}, bf16[512,4096]{1,0:T(8,128)(2,1)}, bf16[4096,512]{1,0:T(8,128)(2,1)}, bf16[40...) custom-call(bf16[1,4096,512]{2,1,0:T(8,128)(2,1)} %x_ref.1, ...), custom_call_target="tpu_custom_call" | custom-call | flops 41875931136 | bytes 68157440 | tf_op jit(solution)/shard_map/tokens/pallas_call | solution.py:100
  61.5 146.9 %reduce.1 = (bf16[1664,512]{1,0:T(8,128)(2,1)}, bf16[512,1664]{1,0:T(8,128)(2,1)}, bf16[512,1664]{1,0:T(8,128)(2,1)}, bf16[3,64,1664]{2,1,0:T(8,128)(2,1)}, bf16...) custom-call(bf16[512,4096]{1,0:T(8,128)(2,1)} %get-tuple-element.53.dyt_ref, ...), custom_call_target="tpu_custom_call" | custom-call | flops 62813896704 | bytes 136314880 | tf_op jit(solution)/shard_map/reduce/pallas_call | solution.py:453
  208.4 1.8 collective-permute-start.3
  210.3 0.3 collective-permute-start.2
  210.5 0.8 collective-permute-start
  211.3 2.5 collective-permute-start.1
  213.8 19.4 %adamw_layer.1 = (bf16[2,512,1664]{2,1,0:T(8,128)(2,1)}, bf16[2,512,1664]{2,1,0:T(8,128)(2,1)}, bf16[2,1664,512]{2,1,0:T(8,128)(2,1)}, f32[2,512,1664]{2,1,0:T(8...) custom-call(f32[16,128]{1,0:T(8,128)} %get-tuple-element.62.sq_ref, ...), custom_call_target="tpu_custom_call" | custom-call | flops 511180800 | bytes 56229888 | tf_op jit(solution)/shard_map/adamw_layer/pallas_call | solution.py:552
  233.2 0.0 collective-permute-done.3.refs_3_
  233.2 0.0 collective-permute-done.2.refs_2_
  233.2 0.1 collective-permute-start.4
  233.3 3.2 %collective-permute-start.5 = (bf16[3,64,1664]{2,1,0:T(8,128)(2,1)}, bf16[3,64,1664]{2,1,0:T(8,128)(2,1)}, u32[]{:S(2)}, u32[]{:S(2)}) collective-permute-start(bf16[3,64,1664]{2,1,0:T(8,128)(2,1)} %collective-permute-done.3.refs_3_), channel_id=1, source_target_pairs={{1,0},{2,1},{3,2},{0,3},{5,4},{6,5},{7,6},{4,7},{9,8},{10,9},{11,1... | collective-permute-start | bytes 1916936 | tf_op jit(solution)/shard_map/ppermute | solution.py:607
  236.5 12.6 %adamw_parts.2 = (bf16[2,512,1664]{2,1,0:T(8,128)(2,1)}, bf16[2,512,1664]{2,1,0:T(8,128)(2,1)}, bf16[2,1664,512]{2,1,0:T(8,128)(2,1)}, f32[2,512,1664]{2,1,0:T(8...) custom-call(s32[8]{0:T(128)} %get-tuple-element.61.places_ref, ...), custom_call_target="tpu_custom_call", output_to_operand_aliasing={{0}: (15, {}), {1}: (16, {}), {2}: (17, {}), {3}: (18, {}),... | custom-call | flops 255590400 | bytes 28114944 | tf_op jit(solution)/shard_map/adamw_parts/pallas_call | solution.py:571
  249.1 0.0 collective-permute-done.refs_0_
  249.1 0.0 collective-permute-done.1.refs_1_
  249.1 3.4 %collective-permute-done.4.refs_2_ = bf16[3,64,1664]{2,1,0:T(8,128)(2,1)} collective-permute-done((bf16[3,64,1664]{2,1,0:T(8,128)(2,1)}, bf16[3,64,1664]{2,1,0:T(8,128)(2,1)}, u32[]{:S(2)}, u32[]{:S(2)}) %collective-permute-start.4) | collective-permute-done | bytes 639008 | tf_op jit(solution)/shard_map/ppermute | solution.py:607
  252.6 0.0 collective-permute-done.5.refs_3_
  252.6 12.6 %adamw_parts.3 = (bf16[2,512,1664]{2,1,0:T(8,128)(2,1)}, bf16[2,512,1664]{2,1,0:T(8,128)(2,1)}, bf16[2,1664,512]{2,1,0:T(8,128)(2,1)}, f32[2,512,1664]{2,1,0:T(8...) custom-call(s32[8]{0:T(128)} %get-tuple-element.61.places_ref, ...), custom_call_target="tpu_custom_call", output_to_operand_aliasing={{0}: (15, {}), {1}: (16, {}), {2}: (17, {}), {3}: (18, {}),... | custom-call | flops 255590400 | bytes 28114944 | tf_op jit(solution)/shard_map/adamw_parts/pallas_call | solution.py:571
Async XLA Ops:
  208.4 24.8 %collective-permute-start.3 = (bf16[3,64,1664]{2,1,0:T(8,128)(2,1)}, bf16[3,64,1664]{2,1,0:T(8,128)(2,1)}, u32[]{:S(2)}, u32[]{:S(2)}) collective-permute-start(bf16[3,64,1664]{2,1,0:T(8,128)(2,1)} %get-tuple-element.63.refs_1_), channel_id=1, source_target_pairs={{1,0},{2,1},{3,2},{0,3},{5,4},{6,5},{7,6},{4,7},{9,8},{10,9},{11,1... | collective-permute-start | bytes 1916936 | tf_op jit(solution)/shard_map/ppermute | solution.py:603
  210.3 23.0 %collective-permute-start.2 = (bf16[3,64,1664]{2,1,0:T(8,128)(2,1)}, bf16[3,64,1664]{2,1,0:T(8,128)(2,1)}, u32[]{:S(2)}, u32[]{:S(2)}) collective-permute-start(bf16[3,64,1664]{2,1,0:T(8,128)(2,1)} %get-tuple-element.64.refs_0_), channel_id=1, source_target_pairs={{0,1},{1,2},{2,3},{3,0},{4,5},{5,6},{6,7},{7,4},{8,9},{9,10},{10,1... | collective-permute-start | bytes 1916936 | tf_op jit(solution)/shard_map/ppermute | solution.py:603
  210.5 38.6 %collective-permute-start = (bf16[3,64,1664]{2,1,0:T(8,128)(2,1)}, bf16[3,64,1664]{2,1,0:T(8,128)(2,1)}, u32[]{:S(2)}, u32[]{:S(2)}) collective-permute-start(bf16[3,64,1664]{2,1,0:T(8,128)(2,1)} %get-tuple-element.63.refs_1_), channel_id=1, source_target_pairs={{0,1},{1,2},{2,3},{3,0},{4,5},{5,6},{6,7},{7,4},{8,9},{9,10},{10,1... | collective-permute-start | bytes 1916936 | tf_op jit(solution)/shard_map/ppermute | solution.py:604
  211.3 37.9 %collective-permute-start.1 = (bf16[3,64,1664]{2,1,0:T(8,128)(2,1)}, bf16[3,64,1664]{2,1,0:T(8,128)(2,1)}, u32[]{:S(2)}, u32[]{:S(2)}) collective-permute-start(bf16[3,64,1664]{2,1,0:T(8,128)(2,1)} %get-tuple-element.64.refs_0_), channel_id=1, source_target_pairs={{1,0},{2,1},{3,2},{0,3},{5,4},{6,5},{7,6},{4,7},{9,8},{10,9},{11,1... | collective-permute-start | bytes 1916936 | tf_op jit(solution)/shard_map/ppermute | solution.py:604
  233.2 19.4 %collective-permute-start.4 = (bf16[3,64,1664]{2,1,0:T(8,128)(2,1)}, bf16[3,64,1664]{2,1,0:T(8,128)(2,1)}, u32[]{:S(2)}, u32[]{:S(2)}) collective-permute-start(bf16[3,64,1664]{2,1,0:T(8,128)(2,1)} %collective-permute-done.2.refs_2_), channel_id=1, source_target_pairs={{0,1},{1,2},{2,3},{3,0},{4,5},{5,6},{6,7},{7,4},{8,9},{9,10},{10,1... | collective-permute-start | bytes 1916936 | tf_op jit(solution)/shard_map/ppermute | solution.py:607
  233.3 19.3 %collective-permute-start.5 = (bf16[3,64,1664]{2,1,0:T(8,128)(2,1)}, bf16[3,64,1664]{2,1,0:T(8,128)(2,1)}, u32[]{:S(2)}, u32[]{:S(2)}) collective-permute-start(bf16[3,64,1664]{2,1,0:T(8,128)(2,1)} %collective-permute-done.3.refs_3_), channel_id=1, source_target_pairs={{1,0},{2,1},{3,2},{0,3},{5,4},{6,5},{7,6},{4,7},{9,8},{10,9},{11,1... | collective-permute-start | bytes 1916936 | tf_op jit(solution)/shard_map/ppermute | solution.py:607

commit v3 on v2

--- a/solution.py
+++ b/solution.py
@@ -13,6 +13,8 @@
 VMEM_LIMIT = 67043328
 TILE = 512
 CHUNK = 4 * LANES
+MOST_ROWS = 192
+RUNS = 4
 
 
 def by_columns(a, b):
@@ -46,15 +48,16 @@
     layers, ff, _ = wd.shape
     blocks = ff // LANES
 
-    @pl.when(pl.program_id(0) == 0)
+    first = pl.program_id(0) == 0
+    loads = [[*side_by_side(wg_ref, wu_ref, wgu.at[n], n, sems.at[n]), pltpu.make_async_copy(wd_ref.at[n], wd.at[n], sems.at[n, 2 * blocks])]
+             for n in range(layers)]
+
+    @pl.when(first)
     def _():
-        copies = []
-        for n in range(layers):
-            copies += side_by_side(wg_ref, wu_ref, wgu.at[n], n, sems.at[n])
-            copies.append(pltpu.make_async_copy(wd_ref.at[n], wd.at[n], sems.at[n, 2 * blocks]))
-        for copy in copies:
-            copy.start()
-        for copy in copies:
+        for copies in loads:
+            for copy in copies:
+                copy.start()
+        for copy in loads[0]:
             copy.wait()
 
     groups = grouped(blocks, many)
@@ -76,6 +79,12 @@
     a1t_ref[...] = a1.T
     dy = dy_ref[...]
     dyt_ref[...] = dy.T
+
+    @pl.when(first)
+    def _():
+        for copy in loads[1]:
+            copy.wait()
+
     for k, count in groups:
         gu = jnp.dot(a1, wgu[1, :, pl.ds(2 * k * LANES, 2 * count * LANES)], preferred_element_type=F32)
         dhid = by_columns(dy, wd[1, pl.ds(k * LANES, count * LANES), :]).astype(BF16).astype(F32)
@@ -133,7 +142,7 @@
                   gd_out, gg_out, gu_out, part_a, part_b, sq_out, places, dgu0_ref,
                   lefts, rights, own_d, own_gu, via_d, via_gu, in_d, in_gu, all_d, all_gu, mine_d, mine_gu, squares,
                   wgu, wd, dgu1_in, keep_in, small_in, dgu0_tile,
-                  left_sem, right_sem, send, recv, sq_send, sq_recv, out_sem, weight_sem, tile_sem, back_sem):
+                  left_sem, right_sem, send, recv, sq_send, sq_recv, out_sem, weight_sem, tile_sem, back_sem, first_sem):
     layers, ff, d = own_d.shape
     tile = dgu0_tile.shape[1]
     tiles = h1_ref.shape[0] // tile
@@ -202,8 +211,9 @@
 
     def each(unit, body):
         down, _, _, size = unit
-        many = 64 if down else 16
-        blocks = (size // 2 if down else d // (2 * n)) // many
+        rows = size // 2 if down else d // (2 * n)
+        many = max(m for m in range(16, MOST_ROWS + 16, 16) if rows % m == 0) if down else rows
+        blocks = rows // many
         for which in range(1 if down else 2):
             def one(i, _, which=which):
                 rows = pl.ds(pl.multiple_of(i * many, many), many)
@@ -245,7 +255,6 @@
 
     seconds = {True: (hid1_ref, hid0_ref), False: (dgu1_ref, dgu0_ref)}
     loads = {
-        (True, layers - 1): pltpu.make_async_copy(dyt_ref, lefts.at[0], left_sem.at[0]),
         (False, layers - 1): pltpu.make_async_copy(a1t_ref, lefts.at[1], left_sem.at[1]),
         (False, 0): pltpu.make_async_copy(a0t_ref, lefts.at[1], left_sem.at[2]),
     }
@@ -336,11 +345,15 @@
         for i in range(max(0, tiles - 2), tiles):
             tile_store(i, i % 2).wait()
 
-    fetch(0, 0, 0).start()
-    loads[(True, layers - 1)].start()
-    loads[(False, layers - 1)].start()
-    for copy in weight_loads + tile_loads(0, 0):
-        copy.start()
+    runs = [pl.ds(k * (tiles * tile // RUNS), tiles * tile // RUNS) for k in range(RUNS)]
+    first_loads = [
+        (pltpu.make_async_copy(dyt_ref.at[:, run], lefts.at[0, :, run], first_sem.at[0, k]),
+         pltpu.make_async_copy(hid1_ref.at[run, pl.ds(0, CHUNK)], rights.at[0, run, :], first_sem.at[1, k]))
+        for k, run in enumerate(runs)
+    ]
+    for pair in first_loads:
+        for copy in pair:
+            copy.start()
 
     done = 0
     half = len(units) // layers
@@ -381,7 +394,21 @@
                     forward_sums(u - 1)
             return 0
 
-        lax.fori_loop(0, count, one, 0)
+        if u == 0:
+            total = None
+            for pair, run in zip(first_loads, runs, strict=True):
+                for copy in pair:
+                    copy.wait()
+                term = jnp.dot(lefts[0, :, run], rights[0, run, :], preferred_element_type=F32)
+                total = term if total is None else total + term
+            fetch(1, 0, 1).start()
+            own_d[layer, pl.ds(0, CHUNK), :] = total.astype(BF16).T
+            loads[(False, layers - 1)].start()
+        else:
+            lax.fori_loop(0, count, one, 0)
+        if u == 2:
+            for copy in weight_loads + tile_loads(0, 0):
+                copy.start()
         done += count
         if u == 0:
             squares[n] = jnp.zeros(squares.shape[1:], F32)
@@ -427,8 +454,9 @@
         parts.append(pltpu.make_async_copy(
             mine_gu.at[:, pl.ds(k * many, many), :], part.at[pl.ds(0, 2)], out_sem.at[3 + k * (blocks + 1) + blocks]))
         parts[-1].start()
-    for k, (owner, side) in enumerate(((me, 0), (me, 1), (left, 0), (right, 1), (left, 1), (right, 0), (far, 0), (far, 1))):
-        places[k] = 2 * owner + side
+    for k, owner in enumerate((me, left, right, far)):
+        places[2 * k] = 2 * owner
+        places[2 * k + 1] = 2 * owner + 1
     for copy in exchange:
         copy.wait_recv()
     total = squares[0]
@@ -494,6 +522,7 @@
             dma((1, 2 * ff // LANES + 1)),
             dma((4, 2)),
             dma((2,)),
+            dma((2, RUNS)),
         ],
         compiler_params=pltpu.CompilerParams(vmem_limit_bytes=VMEM_LIMIT, collective_id=0, has_side_effects=True),
         cost_estimate=pl.CostEstimate(flops=2 * 9 * tokens * d * ff, bytes_accessed=20 * tokens * ff, transcendentals=tokens * ff),
@@ -605,7 +634,7 @@
         new = adamw_layer(squares, (gg, gu, gd), arrays, layers - 1, 4)
         left_a, right_b, *new = lax.optimization_barrier((left_a, right_b, *new))
         far_a, far_b = lax.ppermute(left_a, "dp", onward), lax.ppermute(right_b, "dp", back)
-        for first, some in ((0, (a, b, left_a, right_b)), (4, (left_b, right_a, far_a, far_b))):
+        for first, some in ((0, (a, b)), (2, (left_a, left_b, right_a, right_b)), (6, (far_a, far_b))):
             new = adamw_parts(squares, places, first, some, arrays, new, 0)
         return tuple(new)
 

time: 266 us -> 260 us (0.977)
  waiting for transfers between devices: 3.46 us -> 0.02 us
    ppermute x1, waiting for transfers between devices: 3.45 us -> 0.01 us  [step(): lax.ppermute(left_a, 'dp', onward)]
    pallas_call x2 -> x3, Pallas kernels: 25.2 us -> 27 us  [adamw_parts(): pl.pallas_call(functools.partial(parts_kernel, count, many), grid_spec=pl...]
  transfers between devices with their start and end apart: 6 -> 6, of which waited for: 1 -> 0; matrix products, arithmetic and copies ran while one was open for 0% -> 0% of each run, Pallas kernels for 12% -> 15%
where the time goes in v3:
time: 260 us
  Pallas kernels  250 us (96%)
  starting transfers between devices  8.65 us (3%)
    pallas_call x1, Pallas kernels, reduced(): pl.pallas_call(functools.partial(reduce_kernel, n), out_shape=[jax.ShapeD...  144 us
    pallas_call x1, Pallas kernels, tokens_pass(): pl.pallas_call(functools.partial(tokens_kernel, many=2), grid=(tokens //...  59.1 us
    pallas_call x3, Pallas kernels, adamw_parts(): pl.pallas_call(functools.partial(parts_kernel, count, many), grid_spec=pl...  27 us
    pallas_call x1, Pallas kernels, adamw_layer(): pl.pallas_call(functools.partial(whole_kernel, count), grid=(blocks,), ou...  19.6 us
  transfers between devices with their start and end apart: 6, of which 0 were waited for; matrix products, arithmetic and copies ran while one was open for 0% of the time, Pallas kernels for 15%

profile of v3, /device:TPU:112, one launch (start us, length us, event | category | flops | bytes accessed | tf_op | source)
XLA Modules:
  0.0 259.5 jit_solution(13465602883726731706)
XLA Ops:
  0.6 59.1 %tokens.1 = (bf16[512,4096]{1,0:T(8,128)(2,1)}, bf16[512,4096]{1,0:T(8,128)(2,1)}, bf16[512,4096]{1,0:T(8,128)(2,1)}, bf16[4096,512]{1,0:T(8,128)(2,1)}, bf16[40...) custom-call(bf16[1,4096,512]{2,1,0:T(8,128)(2,1)} %x_ref.1, ...), custom_call_target="tpu_custom_call" | custom-call | flops 41875931136 | bytes 68157440 | tf_op jit(solution)/shard_map/tokens/pallas_call | solution.py:109
  59.7 144.3 %reduce.1 = (bf16[1664,512]{1,0:T(8,128)(2,1)}, bf16[512,1664]{1,0:T(8,128)(2,1)}, bf16[512,1664]{1,0:T(8,128)(2,1)}, bf16[3,64,1664]{2,1,0:T(8,128)(2,1)}, bf16...) custom-call(bf16[512,4096]{1,0:T(8,128)(2,1)} %get-tuple-element.62.dyt_ref, ...), custom_call_target="tpu_custom_call" | custom-call | flops 62813896704 | bytes 136314880 | tf_op jit(solution)/shard_map/reduce/pallas_call | solution.py:481
  204.0 0.9 collective-permute-start
  204.9 2.5 collective-permute-start.1
  207.3 0.5 collective-permute-start.5
  207.8 1.6 collective-permute-start.4
  209.3 19.6 %adamw_layer.1 = (bf16[2,512,1664]{2,1,0:T(8,128)(2,1)}, bf16[2,512,1664]{2,1,0:T(8,128)(2,1)}, bf16[2,1664,512]{2,1,0:T(8,128)(2,1)}, f32[2,512,1664]{2,1,0:T(8...) custom-call(f32[16,128]{1,0:T(8,128)} %get-tuple-element.71.sq_ref, ...), custom_call_target="tpu_custom_call" | custom-call | flops 511180800 | bytes 56229888 | tf_op jit(solution)/shard_map/adamw_layer/pallas_call | solution.py:581
  229.0 0.0 collective-permute-done.refs_0_
  229.0 0.0 collective-permute-done.1.refs_3_
  229.0 0.1 collective-permute-start.2
  229.1 3.2 %collective-permute-start.3 = (bf16[3,64,1664]{2,1,0:T(8,128)(2,1)}, bf16[3,64,1664]{2,1,0:T(8,128)(2,1)}, u32[]{:S(2)}, u32[]{:S(2)}) collective-permute-start(bf16[3,64,1664]{2,1,0:T(8,128)(2,1)} %collective-permute-done.1.refs_3_), channel_id=1, source_target_pairs={{1,0},{2,1},{3,2},{0,3},{5,4},{6,5},{7,6},{4,7},{9,8},{10,9},{11,1... | collective-permute-start | bytes 1916936 | tf_op jit(solution)/shard_map/ppermute | solution.py:636
  232.3 7.1 %adamw_parts.3 = (bf16[2,512,1664]{2,1,0:T(8,128)(2,1)}, bf16[2,512,1664]{2,1,0:T(8,128)(2,1)}, bf16[2,1664,512]{2,1,0:T(8,128)(2,1)}, f32[2,512,1664]{2,1,0:T(8...) custom-call(s32[8]{0:T(128)} %get-tuple-element.70.places_ref, ...), custom_call_target="tpu_custom_call", output_to_operand_aliasing={{0}: (13, {}), {1}: (14, {}), {2}: (15, {}), {3}: (16, {}),... | custom-call | flops 127795200 | bytes 14057472 | tf_op jit(solution)/shard_map/adamw_parts/pallas_call | solution.py:600
  239.4 0.0 collective-permute-done.5.refs_2_
  239.5 0.0 collective-permute-done.4.refs_1_
  239.5 12.7 %adamw_parts.4 = (bf16[2,512,1664]{2,1,0:T(8,128)(2,1)}, bf16[2,512,1664]{2,1,0:T(8,128)(2,1)}, bf16[2,1664,512]{2,1,0:T(8,128)(2,1)}, f32[2,512,1664]{2,1,0:T(8...) custom-call(s32[8]{0:T(128)} %get-tuple-element.70.places_ref, ...), custom_call_target="tpu_custom_call", output_to_operand_aliasing={{0}: (15, {}), {1}: (16, {}), {2}: (17, {}), {3}: (18, {}),... | custom-call | flops 255590400 | bytes 28114944 | tf_op jit(solution)/shard_map/adamw_parts/pallas_call | solution.py:600
  252.1 0.0 collective-permute-done.2.refs_0_
  252.1 0.0 collective-permute-done.3.refs_1_
  252.2 7.2 %adamw_parts.5 = (bf16[2,512,1664]{2,1,0:T(8,128)(2,1)}, bf16[2,512,1664]{2,1,0:T(8,128)(2,1)}, bf16[2,1664,512]{2,1,0:T(8,128)(2,1)}, f32[2,512,1664]{2,1,0:T(8...) custom-call(s32[8]{0:T(128)} %get-tuple-element.70.places_ref, ...), custom_call_target="tpu_custom_call", output_to_operand_aliasing={{0}: (13, {}), {1}: (14, {}), {2}: (15, {}), {3}: (16, {}),... | custom-call | flops 127795200 | bytes 14057472 | tf_op jit(solution)/shard_map/adamw_parts/pallas_call | solution.py:600
Async XLA Ops:
  204.0 25.0 %collective-permute-start = (bf16[3,64,1664]{2,1,0:T(8,128)(2,1)}, bf16[3,64,1664]{2,1,0:T(8,128)(2,1)}, u32[]{:S(2)}, u32[]{:S(2)}) collective-permute-start(bf16[3,64,1664]{2,1,0:T(8,128)(2,1)} %get-tuple-element.72.refs_0_), channel_id=1, source_target_pairs={{0,1},{1,2},{2,3},{3,0},{4,5},{5,6},{6,7},{7,4},{8,9},{9,10},{10,1... | collective-permute-start | bytes 1916936 | tf_op jit(solution)/shard_map/ppermute | solution.py:632
  204.9 24.1 %collective-permute-start.1 = (bf16[3,64,1664]{2,1,0:T(8,128)(2,1)}, bf16[3,64,1664]{2,1,0:T(8,128)(2,1)}, u32[]{:S(2)}, u32[]{:S(2)}) collective-permute-start(bf16[3,64,1664]{2,1,0:T(8,128)(2,1)} %get-tuple-element.73.refs_1_), channel_id=1, source_target_pairs={{1,0},{2,1},{3,2},{0,3},{5,4},{6,5},{7,6},{4,7},{9,8},{10,9},{11,1... | collective-permute-start | bytes 1916936 | tf_op jit(solution)/shard_map/ppermute | solution.py:632
  207.3 32.1 %collective-permute-start.5 = (bf16[3,64,1664]{2,1,0:T(8,128)(2,1)}, bf16[3,64,1664]{2,1,0:T(8,128)(2,1)}, u32[]{:S(2)}, u32[]{:S(2)}) collective-permute-start(bf16[3,64,1664]{2,1,0:T(8,128)(2,1)} %get-tuple-element.72.refs_0_), channel_id=1, source_target_pairs={{1,0},{2,1},{3,2},{0,3},{5,4},{6,5},{7,6},{4,7},{9,8},{10,9},{11,1... | collective-permute-start | bytes 1916936 | tf_op jit(solution)/shard_map/ppermute | solution.py:633
  207.8 31.7 %collective-permute-start.4 = (bf16[3,64,1664]{2,1,0:T(8,128)(2,1)}, bf16[3,64,1664]{2,1,0:T(8,128)(2,1)}, u32[]{:S(2)}, u32[]{:S(2)}) collective-permute-start(bf16[3,64,1664]{2,1,0:T(8,128)(2,1)} %get-tuple-element.73.refs_1_), channel_id=1, source_target_pairs={{0,1},{1,2},{2,3},{3,0},{4,5},{5,6},{6,7},{7,4},{8,9},{9,10},{10,1... | collective-permute-start | bytes 1916936 | tf_op jit(solution)/shard_map/ppermute | solution.py:633
  229.0 23.1 %collective-permute-start.2 = (bf16[3,64,1664]{2,1,0:T(8,128)(2,1)}, bf16[3,64,1664]{2,1,0:T(8,128)(2,1)}, u32[]{:S(2)}, u32[]{:S(2)}) collective-permute-start(bf16[3,64,1664]{2,1,0:T(8,128)(2,1)} %collective-permute-done.refs_0_), channel_id=1, source_target_pairs={{0,1},{1,2},{2,3},{3,0},{4,5},{5,6},{6,7},{7,4},{8,9},{9,10},{10,1... | collective-permute-start | bytes 1916936 | tf_op jit(solution)/shard_map/ppermute | solution.py:636
  229.1 23.0 %collective-permute-start.3 = (bf16[3,64,1664]{2,1,0:T(8,128)(2,1)}, bf16[3,64,1664]{2,1,0:T(8,128)(2,1)}, u32[]{:S(2)}, u32[]{:S(2)}) collective-permute-start(bf16[3,64,1664]{2,1,0:T(8,128)(2,1)} %collective-permute-done.1.refs_3_), channel_id=1, source_target_pairs={{1,0},{2,1},{3,2},{0,3},{5,4},{6,5},{7,6},{4,7},{9,8},{10,9},{11,1... | collective-permute-start | bytes 1916936 | tf_op jit(solution)/shard_map/ppermute | solution.py:636
